TPU v7x, 32 devices: a 4x4x1 block of a 4x4x8 slice. The times are simulated.
32 devices in a mesh: dp: 1 (over z), tp: 4 (over y), pp: 8 (over x, core).
Axes of the slice: x: 4, y: 4, z: 1, core: 2. Of those that a mesh axis runs over, the one named last changes fastest.
The devices are a block of a 4x4x8 slice.
Arguments:
- x_in: bfloat16 [16, 1, 128, 2560], P('dp', None, 'tp')
- ln1_gain: float32 [8, 2560], P('pp')
- ln1_shift: float32 [8, 2560], P('pp')
- w_qkv: bfloat16 [8, 2560, 7680], P('pp', None, 'tp')
- b_qkv: float32 [8, 7680], P('pp', 'tp')
- w_out: bfloat16 [8, 32, 80, 2560], P('pp', 'tp')
- b_out: float32 [8, 2560], P('pp')
- ln2_gain: float32 [8, 2560], P('pp')
- ln2_shift: float32 [8, 2560], P('pp')
- w_up: bfloat16 [8, 2560, 10240], P('pp', None, 'tp')
- b_up: float32 [8, 10240], P('pp', 'tp')
- w_down: bfloat16 [8, 10240, 2560], P('pp', 'tp')
- b_down: float32 [8, 2560], P('pp')
Outputs:
- output: bfloat16 [16, 1, 128, 2560], P(('dp', 'pp'), None, 'tp')
All inputs are finite; a program needn't handle non-finite values.
Results may differ from a plain program's by a relative error of at most 0.02.
Values are sent between devices in bfloat16 or wider.
A program may use at most 768 MiB of HBM per device.

v0:
```python
import jax
import jax.numpy as jnp
from jax import lax
from jax.sharding import PartitionSpec as P

LN_EPS = 1e-5


def layer_norm(act_rows, ln_gain, ln_shift):
    rows_f32 = act_rows.astype(jnp.float32)
    row_mean = jnp.mean(rows_f32, axis=-1, keepdims=True)
    centered = rows_f32 - row_mean
    row_var = jnp.mean(centered * centered, axis=-1, keepdims=True)
    return (centered * lax.rsqrt(row_var + LN_EPS) * ln_gain + ln_shift).astype(jnp.bfloat16)


def causal_attention(qkv, head_dim):
    seq_len = qkv.shape[1]
    scores = jnp.einsum("bqhe,bkhe->bhqk", qkv[:, :, :, 0], qkv[:, :, :, 1],
                        preferred_element_type=jnp.float32) * head_dim ** -0.5
    row_pos = lax.broadcasted_iota(jnp.int32, (seq_len, seq_len), 0)
    col_pos = lax.broadcasted_iota(jnp.int32, (seq_len, seq_len), 1)
    scores = jnp.where(row_pos >= col_pos, scores, -1e30)
    attn_probs = jax.nn.softmax(scores, axis=-1).astype(jnp.bfloat16)
    return jnp.einsum("bhqk,bkhe->bqhe", attn_probs, qkv[:, :, :, 2],
                      preferred_element_type=jnp.float32).astype(jnp.bfloat16)


def stage_layer(act_in, layer_params):
    (ln1_gain, ln1_shift, w_qkv, b_qkv, w_out, b_out,
     ln2_gain, ln2_shift, w_up, b_up, w_down, b_down) = layer_params
    local_heads, head_dim = w_out.shape[0], w_out.shape[1]
    normed = layer_norm(act_in, ln1_gain, ln1_shift)
    gathered = lax.all_gather(normed, "tp", axis=1, tiled=True)
    batch_size, seq_len = gathered.shape[0], gathered.shape[1]
    qkv = (jnp.einsum("bsd,de->bse", gathered, w_qkv, preferred_element_type=jnp.float32) + b_qkv).astype(jnp.bfloat16)
    context = causal_attention(qkv.reshape(batch_size, seq_len, local_heads, 3, head_dim), head_dim)
    attn_part = jnp.einsum("crif,ife->cre", context, w_out, preferred_element_type=jnp.float32).astype(jnp.bfloat16)
    attn_out = lax.psum_scatter(attn_part, "tp", scatter_dimension=1, tiled=True)
    mid_act = (act_in.astype(jnp.float32) + attn_out.astype(jnp.float32) + b_out).astype(jnp.bfloat16)
    normed_mid = layer_norm(mid_act, ln2_gain, ln2_shift)
    gathered_mid = lax.all_gather(normed_mid, "tp", axis=1, tiled=True)
    hidden = jax.nn.relu(jnp.einsum("bsd,df->bsf", gathered_mid, w_up, preferred_element_type=jnp.float32) + b_up).astype(jnp.bfloat16)
    down_part = jnp.einsum("bsf,fd->bsd", hidden, w_down, preferred_element_type=jnp.float32).astype(jnp.bfloat16)
    down_out = lax.psum_scatter(down_part, "tp", scatter_dimension=1, tiled=True)
    return (mid_act.astype(jnp.float32) + down_out.astype(jnp.float32) + b_down).astype(jnp.bfloat16)


def solution(mesh):
    pp_size = mesh.shape["pp"]
    send_next = [(src_idx, src_idx + 1) for src_idx in range(pp_size - 1)]
    in_specs = (P("dp", None, "tp", None),
                P("pp", None), P("pp", None), P("pp", None, "tp"), P("pp", "tp"),
                P("pp", "tp", None, None), P("pp", None), P("pp", None), P("pp", None),
                P("pp", None, "tp"), P("pp", "tp"), P("pp", "tp", None), P("pp", None))
    out_specs = P(("dp", "pp"), None, "tp", None)

    def device_program(x_local, *stage_args):
        layer_params = tuple(stacked_arr[0] for stacked_arr in stage_args)
        num_micro = x_local.shape[0]
        per_stage = num_micro // pp_size
        stage_idx = lax.axis_index("pp")
        is_first = stage_idx == 0
        is_last = stage_idx == pp_size - 1

        def tick_body(tick_idx, loop_state):
            incoming, collected = loop_state
            micro_idx = tick_idx - stage_idx
            safe_idx = jnp.clip(micro_idx, 0, num_micro - 1)
            fresh = lax.dynamic_index_in_dim(x_local, safe_idx, 0, keepdims=False)
            layer_in = jnp.where(is_first, fresh, incoming)
            layer_out = stage_layer(layer_in, layer_params)
            keep = is_last & (micro_idx >= 0) & (micro_idx < num_micro)
            previous = lax.dynamic_index_in_dim(collected, safe_idx, 0, keepdims=False)
            collected = lax.dynamic_update_index_in_dim(collected, jnp.where(keep, layer_out, previous), safe_idx, 0)
            incoming = lax.ppermute(layer_out, "pp", perm=send_next)
            return incoming, collected

        init_state = (jnp.zeros_like(x_local[0]), jnp.zeros_like(x_local))
        collected = lax.fori_loop(0, num_micro + pp_size - 1, tick_body, init_state)[1]
        own_block = collected[(pp_size - 1) * per_stage:]
        result = jnp.where(is_last, own_block, jnp.zeros_like(own_block))
        for dest_idx in range(pp_size - 1):
            out_block = collected[dest_idx * per_stage:(dest_idx + 1) * per_stage]
            result = result + lax.ppermute(out_block, "pp", perm=[(pp_size - 1, dest_idx)])
        return result

    return jax.shard_map(device_program, mesh=mesh, in_specs=in_specs, out_specs=out_specs, check_vma=False)
```

profile of v0, /device:TPU:103, one launch (start us, length us, event | category | flops | bytes accessed | tf_op | source)
XLA Modules:
  0.0 2423.9 jit_solution(3535855729810630494)
XLA Ops:
  8.4 2383.0 %while.15 = (s32[]{:T(128)}, bf16[1,32,2560]{2,1,0:T(8,128)(2,1)S(1)}, bf16[16,1,32,2560]{3,2,1,0:T(8,128)(2,1)}, pred[]{:T(512)}, s32[]{:T(128)}, /*index=5*/bf...) while((s32[]{:T(128)}, ...), condition=%wide.region_9.10_spmd, body=%wide.region_0.9_spmd.sunk | while | flops 5081071616 | bytes 68668632 | solution.py:80
  10.8 13.4 all_gather.16
  37.9 20.0 reduce-scatter.3.cloned.1.call-done
  85.2 19.7 reduce-scatter.5.cloned.1.call-done
  139.2 22.3 reduce-scatter.3.cloned.1.call-done
  174.7 12.9 fusion.72
  188.6 19.8 reduce-scatter.5.cloned.1.call-done
  242.9 22.2 reduce-scatter.3.cloned.1.call-done
  292.3 19.7 reduce-scatter.5.cloned.1.call-done
  346.4 22.3 reduce-scatter.3.cloned.1.call-done
  381.8 12.9 fusion.72
  395.7 19.9 reduce-scatter.5.cloned.1.call-done
  449.9 22.3 reduce-scatter.3.cloned.1.call-done
  499.5 19.8 reduce-scatter.5.cloned.1.call-done
  553.6 22.2 reduce-scatter.3.cloned.1.call-done
  589.0 12.9 fusion.72
  603.0 19.8 reduce-scatter.5.cloned.1.call-done
  657.1 22.3 reduce-scatter.3.cloned.1.call-done
  692.7 12.9 fusion.72
  706.6 19.7 reduce-scatter.5.cloned.1.call-done
  760.7 22.3 reduce-scatter.3.cloned.1.call-done
  796.3 12.9 fusion.72
  810.3 19.7 reduce-scatter.5.cloned.1.call-done
  864.3 22.2 reduce-scatter.3.cloned.1.call-done
  899.9 12.9 fusion.72
  913.8 19.7 reduce-scatter.5.cloned.1.call-done
  967.9 22.3 reduce-scatter.3.cloned.1.call-done
  1003.5 12.9 fusion.72
  1017.5 19.6 reduce-scatter.5.cloned.1.call-done
  1071.5 22.2 reduce-scatter.3.cloned.1.call-done
  1107.1 12.9 fusion.72
  1121.0 19.7 reduce-scatter.5.cloned.1.call-done
  1175.1 22.2 reduce-scatter.3.cloned.1.call-done
  1224.5 19.7 reduce-scatter.5.cloned.1.call-done
  1278.7 22.2 reduce-scatter.3.cloned.1.call-done
  1314.1 12.9 fusion.72
  1328.1 19.8 reduce-scatter.5.cloned.1.call-done
  1382.2 22.2 reduce-scatter.3.cloned.1.call-done
  1417.7 12.9 fusion.72
  1431.7 19.7 reduce-scatter.5.cloned.1.call-done
  1485.8 22.2 reduce-scatter.3.cloned.1.call-done
  1535.3 19.8 reduce-scatter.5.cloned.1.call-done
  1589.4 22.3 reduce-scatter.3.cloned.1.call-done
  1624.9 12.9 fusion.72
  1638.8 19.8 reduce-scatter.5.cloned.1.call-done
  1693.0 22.2 reduce-scatter.3.cloned.1.call-done
  1742.5 19.7 reduce-scatter.5.cloned.1.call-done
  1796.6 22.3 reduce-scatter.3.cloned.1.call-done
  1832.2 12.9 fusion.72
  1846.2 19.6 reduce-scatter.5.cloned.1.call-done
  1900.2 22.2 reduce-scatter.3.cloned.1.call-done
  1949.6 19.8 reduce-scatter.5.cloned.1.call-done
  2003.8 22.2 reduce-scatter.3.cloned.1.call-done
  2039.3 12.9 fusion.72
  2053.3 19.7 reduce-scatter.5.cloned.1.call-done
  2107.3 22.3 reduce-scatter.3.cloned.1.call-done
  2142.8 12.9 fusion.72
  2156.8 19.7 reduce-scatter.5.cloned.1.call-done
  2210.9 22.3 reduce-scatter.3.cloned.1.call-done
  2246.4 12.9 fusion.72
  2260.4 19.8 reduce-scatter.5.cloned.1.call-done
  2314.5 22.3 reduce-scatter.3.cloned.1.call-done
  2350.1 12.9 fusion.72
  2364.0 19.8 reduce-scatter.5.cloned.1.call-done
  (843 shorter events, 1224.4 us)
Async XLA Ops:
  8.4 49.5 %reduce-scatter.3.cloned.1.call-start = ((), (), s32[]{:S(2)}) async-start(), calls=%async_computation.2 | async-start | bytes 819200 | tf_op jit(solution)/shard_map/while/body/eval_jaxpr/reduce_scatter | solution.py:39
  37.7 67.2 %reduce-scatter.5.cloned.1.call-start = ((), (), s32[]{:S(2)}) async-start(), calls=%async_computation.3 | async-start | bytes 819200 | tf_op jit(solution)/shard_map/while/body/eval_jaxpr/reduce_scatter | solution.py:45
  106.5 6.0 collective-permute-start
  112.5 49.0 %reduce-scatter.3.cloned.1.call-start = ((), (), s32[]{:S(2)}) async-start(), calls=%async_computation.2 | async-start | bytes 819200 | tf_op jit(solution)/shard_map/while/body/eval_jaxpr/reduce_scatter | solution.py:39
  139.0 69.4 %reduce-scatter.5.cloned.1.call-start = ((), (), s32[]{:S(2)}) async-start(), calls=%async_computation.3 | async-start | bytes 819200 | tf_op jit(solution)/shard_map/while/body/eval_jaxpr/reduce_scatter | solution.py:45
  210.1 6.0 collective-permute-start
  216.1 49.0 %reduce-scatter.3.cloned.1.call-start = ((), (), s32[]{:S(2)}) async-start(), calls=%async_computation.2 | async-start | bytes 819200 | tf_op jit(solution)/shard_map/while/body/eval_jaxpr/reduce_scatter | solution.py:39
  242.6 69.4 %reduce-scatter.5.cloned.1.call-start = ((), (), s32[]{:S(2)}) async-start(), calls=%async_computation.3 | async-start | bytes 819200 | tf_op jit(solution)/shard_map/while/body/eval_jaxpr/reduce_scatter | solution.py:45
  319.6 49.0 %reduce-scatter.3.cloned.1.call-start = ((), (), s32[]{:S(2)}) async-start(), calls=%async_computation.2 | async-start | bytes 819200 | tf_op jit(solution)/shard_map/while/body/eval_jaxpr/reduce_scatter | solution.py:39
  346.1 69.5 %reduce-scatter.5.cloned.1.call-start = ((), (), s32[]{:S(2)}) async-start(), calls=%async_computation.3 | async-start | bytes 819200 | tf_op jit(solution)/shard_map/while/body/eval_jaxpr/reduce_scatter | solution.py:45
  423.2 49.0 %reduce-scatter.3.cloned.1.call-start = ((), (), s32[]{:S(2)}) async-start(), calls=%async_computation.2 | async-start | bytes 819200 | tf_op jit(solution)/shard_map/while/body/eval_jaxpr/reduce_scatter | solution.py:39
  449.7 69.5 %reduce-scatter.5.cloned.1.call-start = ((), (), s32[]{:S(2)}) async-start(), calls=%async_computation.3 | async-start | bytes 819200 | tf_op jit(solution)/shard_map/while/body/eval_jaxpr/reduce_scatter | solution.py:45
  526.8 49.0 %reduce-scatter.3.cloned.1.call-start = ((), (), s32[]{:S(2)}) async-start(), calls=%async_computation.2 | async-start | bytes 819200 | tf_op jit(solution)/shard_map/while/body/eval_jaxpr/reduce_scatter | solution.py:39
  553.4 69.4 %reduce-scatter.5.cloned.1.call-start = ((), (), s32[]{:S(2)}) async-start(), calls=%async_computation.3 | async-start | bytes 819200 | tf_op jit(solution)/shard_map/while/body/eval_jaxpr/reduce_scatter | solution.py:45
  624.4 6.0 collective-permute-start
  630.4 49.0 %reduce-scatter.3.cloned.1.call-start = ((), (), s32[]{:S(2)}) async-start(), calls=%async_computation.2 | async-start | bytes 819200 | tf_op jit(solution)/shard_map/while/body/eval_jaxpr/reduce_scatter | solution.py:39
  656.9 69.4 %reduce-scatter.5.cloned.1.call-start = ((), (), s32[]{:S(2)}) async-start(), calls=%async_computation.3 | async-start | bytes 819200 | tf_op jit(solution)/shard_map/while/body/eval_jaxpr/reduce_scatter | solution.py:45
  734.0 49.0 %reduce-scatter.3.cloned.1.call-start = ((), (), s32[]{:S(2)}) async-start(), calls=%async_computation.2 | async-start | bytes 819200 | tf_op jit(solution)/shard_map/while/body/eval_jaxpr/reduce_scatter | solution.py:39
  760.5 69.5 %reduce-scatter.5.cloned.1.call-start = ((), (), s32[]{:S(2)}) async-start(), calls=%async_computation.3 | async-start | bytes 819200 | tf_op jit(solution)/shard_map/while/body/eval_jaxpr/reduce_scatter | solution.py:45
  837.6 48.9 %reduce-scatter.3.cloned.1.call-start = ((), (), s32[]{:S(2)}) async-start(), calls=%async_computation.2 | async-start | bytes 819200 | tf_op jit(solution)/shard_map/while/body/eval_jaxpr/reduce_scatter | solution.py:39
  864.1 69.4 %reduce-scatter.5.cloned.1.call-start = ((), (), s32[]{:S(2)}) async-start(), calls=%async_computation.3 | async-start | bytes 819200 | tf_op jit(solution)/shard_map/while/body/eval_jaxpr/reduce_scatter | solution.py:45
  941.2 49.0 %reduce-scatter.3.cloned.1.call-start = ((), (), s32[]{:S(2)}) async-start(), calls=%async_computation.2 | async-start | bytes 819200 | tf_op jit(solution)/shard_map/while/body/eval_jaxpr/reduce_scatter | solution.py:39
  967.7 69.5 %reduce-scatter.5.cloned.1.call-start = ((), (), s32[]{:S(2)}) async-start(), calls=%async_computation.3 | async-start | bytes 819200 | tf_op jit(solution)/shard_map/while/body/eval_jaxpr/reduce_scatter | solution.py:45
  1038.8 6.0 collective-permute-start
  1044.8 49.0 %reduce-scatter.3.cloned.1.call-start = ((), (), s32[]{:S(2)}) async-start(), calls=%async_computation.2 | async-start | bytes 819200 | tf_op jit(solution)/shard_map/while/body/eval_jaxpr/reduce_scatter | solution.py:39
  1071.3 69.4 %reduce-scatter.5.cloned.1.call-start = ((), (), s32[]{:S(2)}) async-start(), calls=%async_computation.3 | async-start | bytes 819200 | tf_op jit(solution)/shard_map/while/body/eval_jaxpr/reduce_scatter | solution.py:45
  1148.3 48.9 %reduce-scatter.3.cloned.1.call-start = ((), (), s32[]{:S(2)}) async-start(), calls=%async_computation.2 | async-start | bytes 819200 | tf_op jit(solution)/shard_map/while/body/eval_jaxpr/reduce_scatter | solution.py:39
  1174.9 69.4 %reduce-scatter.5.cloned.1.call-start = ((), (), s32[]{:S(2)}) async-start(), calls=%async_computation.3 | async-start | bytes 819200 | tf_op jit(solution)/shard_map/while/body/eval_jaxpr/reduce_scatter | solution.py:45
  1245.9 6.0 collective-permute-start
  1251.9 48.9 %reduce-scatter.3.cloned.1.call-start = ((), (), s32[]{:S(2)}) async-start(), calls=%async_computation.2 | async-start | bytes 819200 | tf_op jit(solution)/shard_map/while/body/eval_jaxpr/reduce_scatter | solution.py:39
  1278.4 69.4 %reduce-scatter.5.cloned.1.call-start = ((), (), s32[]{:S(2)}) async-start(), calls=%async_computation.3 | async-start | bytes 819200 | tf_op jit(solution)/shard_map/while/body/eval_jaxpr/reduce_scatter | solution.py:45
  1349.5 6.0 collective-permute-start
  1355.5 49.0 %reduce-scatter.3.cloned.1.call-start = ((), (), s32[]{:S(2)}) async-start(), calls=%async_computation.2 | async-start | bytes 819200 | tf_op jit(solution)/shard_map/while/body/eval_jaxpr/reduce_scatter | solution.py:39
  1382.0 69.4 %reduce-scatter.5.cloned.1.call-start = ((), (), s32[]{:S(2)}) async-start(), calls=%async_computation.3 | async-start | bytes 819200 | tf_op jit(solution)/shard_map/while/body/eval_jaxpr/reduce_scatter | solution.py:45
  1453.1 6.0 collective-permute-start
  1459.1 49.0 %reduce-scatter.3.cloned.1.call-start = ((), (), s32[]{:S(2)}) async-start(), calls=%async_computation.2 | async-start | bytes 819200 | tf_op jit(solution)/shard_map/while/body/eval_jaxpr/reduce_scatter | solution.py:39
  1485.6 69.4 %reduce-scatter.5.cloned.1.call-start = ((), (), s32[]{:S(2)}) async-start(), calls=%async_computation.3 | async-start | bytes 819200 | tf_op jit(solution)/shard_map/while/body/eval_jaxpr/reduce_scatter | solution.py:45
  1556.7 6.0 collective-permute-start
  1562.7 49.0 %reduce-scatter.3.cloned.1.call-start = ((), (), s32[]{:S(2)}) async-start(), calls=%async_computation.2 | async-start | bytes 819200 | tf_op jit(solution)/shard_map/while/body/eval_jaxpr/reduce_scatter | solution.py:39
  1589.2 69.4 %reduce-scatter.5.cloned.1.call-start = ((), (), s32[]{:S(2)}) async-start(), calls=%async_computation.3 | async-start | bytes 819200 | tf_op jit(solution)/shard_map/while/body/eval_jaxpr/reduce_scatter | solution.py:45
  1660.3 6.0 collective-permute-start
  1666.3 49.0 %reduce-scatter.3.cloned.1.call-start = ((), (), s32[]{:S(2)}) async-start(), calls=%async_computation.2 | async-start | bytes 819200 | tf_op jit(solution)/shard_map/while/body/eval_jaxpr/reduce_scatter | solution.py:39
  1692.8 69.4 %reduce-scatter.5.cloned.1.call-start = ((), (), s32[]{:S(2)}) async-start(), calls=%async_computation.3 | async-start | bytes 819200 | tf_op jit(solution)/shard_map/while/body/eval_jaxpr/reduce_scatter | solution.py:45
  1769.9 49.0 %reduce-scatter.3.cloned.1.call-start = ((), (), s32[]{:S(2)}) async-start(), calls=%async_computation.2 | async-start | bytes 819200 | tf_op jit(solution)/shard_map/while/body/eval_jaxpr/reduce_scatter | solution.py:39
  1796.3 69.5 %reduce-scatter.5.cloned.1.call-start = ((), (), s32[]{:S(2)}) async-start(), calls=%async_computation.3 | async-start | bytes 819200 | tf_op jit(solution)/shard_map/while/body/eval_jaxpr/reduce_scatter | solution.py:45
  1873.5 48.9 %reduce-scatter.3.cloned.1.call-start = ((), (), s32[]{:S(2)}) async-start(), calls=%async_computation.2 | async-start | bytes 819200 | tf_op jit(solution)/shard_map/while/body/eval_jaxpr/reduce_scatter | solution.py:39
  1900.0 69.4 %reduce-scatter.5.cloned.1.call-start = ((), (), s32[]{:S(2)}) async-start(), calls=%async_computation.3 | async-start | bytes 819200 | tf_op jit(solution)/shard_map/while/body/eval_jaxpr/reduce_scatter | solution.py:45
  1971.0 6.0 collective-permute-start
  1977.0 49.0 %reduce-scatter.3.cloned.1.call-start = ((), (), s32[]{:S(2)}) async-start(), calls=%async_computation.2 | async-start | bytes 819200 | tf_op jit(solution)/shard_map/while/body/eval_jaxpr/reduce_scatter | solution.py:39
  2003.6 69.4 %reduce-scatter.5.cloned.1.call-start = ((), (), s32[]{:S(2)}) async-start(), calls=%async_computation.3 | async-start | bytes 819200 | tf_op jit(solution)/shard_map/while/body/eval_jaxpr/reduce_scatter | solution.py:45
  2074.6 6.0 collective-permute-start
  2080.6 49.0 %reduce-scatter.3.cloned.1.call-start = ((), (), s32[]{:S(2)}) async-start(), calls=%async_computation.2 | async-start | bytes 819200 | tf_op jit(solution)/shard_map/while/body/eval_jaxpr/reduce_scatter | solution.py:39
  2107.1 69.4 %reduce-scatter.5.cloned.1.call-start = ((), (), s32[]{:S(2)}) async-start(), calls=%async_computation.3 | async-start | bytes 819200 | tf_op jit(solution)/shard_map/while/body/eval_jaxpr/reduce_scatter | solution.py:45
  2184.2 49.0 %reduce-scatter.3.cloned.1.call-start = ((), (), s32[]{:S(2)}) async-start(), calls=%async_computation.2 | async-start | bytes 819200 | tf_op jit(solution)/shard_map/while/body/eval_jaxpr/reduce_scatter | solution.py:39
  2210.7 69.5 %reduce-scatter.5.cloned.1.call-start = ((), (), s32[]{:S(2)}) async-start(), calls=%async_computation.3 | async-start | bytes 819200 | tf_op jit(solution)/shard_map/while/body/eval_jaxpr/reduce_scatter | solution.py:45
  2287.8 49.0 %reduce-scatter.3.cloned.1.call-start = ((), (), s32[]{:S(2)}) async-start(), calls=%async_computation.2 | async-start | bytes 819200 | tf_op jit(solution)/shard_map/while/body/eval_jaxpr/reduce_scatter | solution.py:39
  2314.3 69.5 %reduce-scatter.5.cloned.1.call-start = ((), (), s32[]{:S(2)}) async-start(), calls=%async_computation.3 | async-start | bytes 819200 | tf_op jit(solution)/shard_map/while/body/eval_jaxpr/reduce_scatter | solution.py:45
  2393.2 10.5 collective-permute-start.1
  2394.8 10.2 collective-permute-start.7
  2399.7 6.7 collective-permute-start.6
  2401.0 7.5 collective-permute-start.5
  2402.4 9.7 collective-permute-start.4
  2403.7 11.8 collective-permute-start.3
  2405.0 10.5 collective-permute-start.2
  (42 other events, 326.7 us)
Sparse Core Ops, SparseCore 0:
  37.8 20.0 reduce-scatter.2
  84.3 20.4 reduce-scatter.4
  139.1 22.3 reduce-scatter.2
  187.8 20.6 reduce-scatter.4
  242.8 22.2 reduce-scatter.2
  291.4 20.5 reduce-scatter.4
  346.3 22.3 reduce-scatter.2
  394.9 20.6 reduce-scatter.4
  449.8 22.3 reduce-scatter.2
  498.6 20.5 reduce-scatter.4
  553.5 22.2 reduce-scatter.2
  602.1 20.6 reduce-scatter.4
  657.0 22.3 reduce-scatter.2
  705.8 20.5 reduce-scatter.4
  760.6 22.3 reduce-scatter.2
  809.4 20.4 reduce-scatter.4
  864.2 22.2 reduce-scatter.2
  912.9 20.5 reduce-scatter.4
  967.8 22.3 reduce-scatter.2
  1016.6 20.4 reduce-scatter.4
  1071.4 22.2 reduce-scatter.2
  1120.1 20.4 reduce-scatter.4
  1175.0 22.2 reduce-scatter.2
  1223.6 20.5 reduce-scatter.4
  1278.6 22.2 reduce-scatter.2
  1327.2 20.5 reduce-scatter.4
  1382.1 22.2 reduce-scatter.2
  1430.8 20.5 reduce-scatter.4
  1485.7 22.2 reduce-scatter.2
  1534.4 20.5 reduce-scatter.4
  1589.3 22.3 reduce-scatter.2
  1638.0 20.5 reduce-scatter.4
  1692.9 22.2 reduce-scatter.2
  1741.6 20.5 reduce-scatter.4
  1796.5 22.3 reduce-scatter.2
  1845.3 20.4 reduce-scatter.4
  1900.1 22.2 reduce-scatter.2
  1948.7 20.6 reduce-scatter.4
  2003.7 22.2 reduce-scatter.2
  2052.4 20.4 reduce-scatter.4
  2107.2 22.3 reduce-scatter.2
  2155.9 20.5 reduce-scatter.4
  2210.8 22.3 reduce-scatter.2
  2259.5 20.6 reduce-scatter.4
  2314.4 22.3 reduce-scatter.2
  2363.2 20.5 reduce-scatter.4
where the time goes:
time: 2430 us; the launch traced here: 2420 us
  waiting for transfers between devices  1080 us (44%)
  matrix products  558 us (23%)
  blocking collectives  522 us (21%)
  other arithmetic  129 us (5%)
  local copies, waits for them, and re-layouts  71.5 us (3%)
  starting transfers between devices  44.5 us (2%)
    reduce_scatter x23, waiting for transfers between devices, stage_layer(): lax.psum_scatter(attn_part, 'tp', scatter_dimension=1, tiled=True)  509 us
    reduce_scatter x23, waiting for transfers between devices, stage_layer(): lax.psum_scatter(down_part, 'tp', scatter_dimension=1, tiled=True)  454 us
    dot_general x23, matrix products, stage_layer(): jnp.einsum('bsf,fd->bsd', hidden, w_down, preferred_element_type=jnp.floa...  297 us
    all_gather x23, blocking collectives, stage_layer(): gathered_mid = lax.all_gather(normed_mid, 'tp', axis=1, tiled=True)  272 us
    all_gather x23, blocking collectives, stage_layer(): gathered = lax.all_gather(normed, 'tp', axis=1, tiled=True)  250 us
    dot_general x23, matrix products, stage_layer(): jnp.einsum('bsd,de->bse', gathered, w_qkv, preferred_element_type=jnp.flo...  146 us
    ppermute x23, waiting for transfers between devices, tick_body(): incoming = lax.ppermute(layer_out, 'pp', perm=send_next)  108 us
    dot_general x23, matrix products, stage_layer(): jnp.einsum('crif,ife->cre', context, w_out, preferred_element_type=jnp.fl...  66.1 us
  transfers between devices with their start and end apart: 76, of which 72 were waited for; matrix products, arithmetic and copies ran while one was open for 1% of the time, Pallas kernels for 0%

commit v1 on v0

v1 whole, which is shorter than its diff:
```python
import functools

import jax
import jax.numpy as jnp
from jax import lax
from jax.experimental import pallas as pl
from jax.experimental.pallas import tpu as pltpu
from jax.sharding import PartitionSpec as P

LN_EPS = 1e-5
MESH = pl.DeviceIdType.MESH
F32 = jnp.float32
BF16 = jnp.bfloat16


def norm_rows(rows, gain, shift):
    rows = rows.astype(F32)
    centered = rows - jnp.mean(rows, axis=-1, keepdims=True)
    var = jnp.mean(centered * centered, axis=-1, keepdims=True)
    return (centered * lax.rsqrt(var + LN_EPS) * gain + shift).astype(BF16)


def layer_kernel(
    num_stages, ring, head_dim,
    x_hbm, g1_ref, s1_ref, wqkv_hbm, bqkv_ref, wout_hbm, bout_ref,
    g2_ref, s2_ref, wup_hbm, bup_ref, wdn_hbm, bdn_ref,
    out_ref,
    wqkv, wout, wup, wdn,
    xs, xf, nb, qkv, cf, acc, x1, hid, part, rl_in, rl_out, fin, x2, obuf,
    w_sem, wg_send, wg_recv, xs_sem, ax_send, ax_recv, ac_send, ac_recv,
    rs_send, rs_recv, pp_send, o_sem, turn_sem,
):
    num_micro, shard, width = x_hbm.shape
    seq = shard * ring
    per_stage = num_micro // num_stages
    own_k = wout_hbm.shape[0]
    qkv_w = wqkv_hbm.shape[1]
    heads = own_k // head_dim
    half = width // 2
    last = num_stages - 1

    me = lax.axis_index("tp")
    stage = lax.axis_index("pp")
    right = lax.rem(me + 1, ring)
    left = lax.rem(me + ring - 1, ring)
    opp = lax.rem(me + 2, ring)
    to_right, to_left = {"tp": right}, {"tp": left}

    def rows_of(owner, n):
        return pl.ds(pl.multiple_of(owner * n, n), n)

    barrier = pltpu.get_barrier_semaphore()

    def greet(device):
        pl.semaphore_signal(barrier, inc=1, device_id=device, device_id_type=MESH)

    greet(to_right)
    greet(to_left)
    pl.when(stage > 0)(lambda: greet({"pp": stage - 1}))
    pl.when(stage < last)(lambda: greet({"pp": stage + 1}))
    pl.when(stage < last - 1)(lambda: greet({"pp": last}))

    @pl.when(stage == last)
    def _():
        for q in range(last - 1):
            greet({"pp": q})

    own_rows = rows_of(me, own_k)
    load_out = pltpu.make_async_copy(wout_hbm, wout.at[own_rows], w_sem.at[0])
    load_qkv = pltpu.make_async_copy(wqkv_hbm, wqkv, w_sem.at[1])
    load_up = pltpu.make_async_copy(wup_hbm, wup, w_sem.at[2])
    load_dn = pltpu.make_async_copy(wdn_hbm, wdn, w_sem.at[3])
    load_out.start()

    def load_x(i):
        return pltpu.make_async_copy(x_hbm.at[i], xs.at[i], xs_sem.at[i])

    @pl.when(stage == 0)
    def _():
        lax.fori_loop(0, num_micro, lambda i, c: (load_x(i).start(), c)[1], 0)

    load_qkv.start()
    load_up.start()
    load_dn.start()

    n_greet = (
        2
        + jnp.where(stage > 0, 1, 0)
        + jnp.where(stage < last, 1, 0)
        + jnp.where(stage < last - 1, 1, 0)
        + jnp.where(stage == last, last - 1, 0)
    )
    pl.semaphore_wait(barrier, n_greet)

    class Gather:
        def __init__(self, own, piece, send, recv):
            self.own, self.piece, self.send, self.recv = own, piece, send, recv

        def copy(self, k, src, owner, h, device):
            return pltpu.make_async_remote_copy(
                src_ref=src, dst_ref=self.piece(owner, h),
                send_sem=self.send.at[k], recv_sem=self.recv.at[k],
                device_id=device, device_id_type=MESH,
            )

        def hop1(self):
            return [
                self.copy(0, self.own(0), me, 0, to_right),
                self.copy(3, self.own(1), me, 1, to_left),
                self.copy(1, self.own(1), me, 1, to_right),
                self.copy(2, self.own(0), me, 0, to_left),
            ]

        def start(self):
            for c in self.hop1():
                c.start()

        def fwd(self):
            return (
                self.copy(4, self.piece(left, 0), left, 0, to_right),
                self.copy(5, self.piece(right, 1), right, 1, to_left),
            )

        def recv_wait(self, k, owner, h):
            self.copy(k, self.piece(owner, h), owner, h, to_right).wait_recv()

        def forward(self):
            a, b = self.fwd()
            self.recv_wait(0, left, 0)
            a.start()
            self.recv_wait(3, right, 1)
            b.start()

        def near(self):
            self.recv_wait(1, left, 1)
            self.recv_wait(2, right, 0)

        def far(self):
            self.recv_wait(4, opp, 0)
            self.recv_wait(5, opp, 1)
            for c in self.hop1():
                c.wait_send()
            for c in self.fwd():
                c.wait_send()

    wk = own_k // 2

    def w_piece(owner, h):
        return wout.at[pl.ds(pl.multiple_of(owner * own_k + h * wk, wk), wk)]

    gather_w = Gather(lambda h: w_piece(me, h), w_piece, wg_send, wg_recv)

    xh = shard // 2
    ch = seq // 2

    def gather_x(i):
        slot = lax.rem(i, 2)

        def piece(owner, h):
            return xf.at[slot, pl.ds(pl.multiple_of(owner * shard + h * xh, xh), xh)]

        def own(h):
            return xs.at[i, pl.ds(h * xh, xh)]

        return Gather(own, piece, ax_send.at[slot], ax_recv.at[slot])

    def gather_c(i):
        slot = lax.rem(i, 2)

        def piece(owner, h):
            return cf.at[slot, owner, pl.ds(h * ch, ch)]

        return Gather(lambda h: piece(me, h), piece, ac_send.at[slot], ac_recv.at[slot])

    def scatter(i):
        slot = lax.rem(i, 2)

        def mine(owner, h):
            return part.at[slot, rows_of(owner, shard), pl.ds(h * half, half)]

        def copy(k, src, dst, device):
            return pltpu.make_async_remote_copy(
                src_ref=src, dst_ref=dst, send_sem=rs_send.at[slot, k], recv_sem=rs_recv.at[slot, k],
                device_id=device, device_id_type=MESH,
            )

        first = [
            copy(0, mine(opp, 0), rl_in.at[slot, 0], to_right),
            copy(1, mine(opp, 1), rl_in.at[slot, 1], to_left),
            copy(2, mine(right, 1), fin.at[slot, 0], to_right),
            copy(3, mine(left, 0), fin.at[slot, 1], to_left),
        ]
        second = [
            copy(4, rl_out.at[slot, 0], fin.at[slot, 2], to_right),
            copy(5, rl_out.at[slot, 1], fin.at[slot, 3], to_left),
        ]
        return slot, mine, first, second

    def scatter_start(i):
        for c in scatter(i)[2]:
            c.start()

    def scatter_relay(i):
        slot, mine, first, second = scatter(i)
        for h, owner in ((0, right), (1, left)):
            first[h].wait_recv()
            rl_out[slot, h] = (rl_in[slot, h].astype(F32) + mine(owner, h)[...].astype(F32)).astype(BF16)
            second[h].start()

    def scatter_finish(i):
        slot, mine, first, second = scatter(i)
        first[2].wait_recv()
        first[3].wait_recv()
        second[0].wait_recv()
        second[1].wait_recv()
        sums = []
        for h, (a, b) in ((0, (1, 2)), (1, (0, 3))):
            sums.append(mine(me, h)[...].astype(F32) + fin[slot, a].astype(F32) + fin[slot, b].astype(F32))
        for c in (*first, *second):
            c.wait_send()
        return sums

    def x_arrival(i):
        load_x(i).wait()

    def ln_shard(i, owner):
        at = rows_of(owner, shard)
        nb[at] = norm_rows(xf[lax.rem(i, 2), at], g1_ref[...], s1_ref[...])

    row_pos = lax.broadcasted_iota(jnp.int32, (seq, seq), 0)
    col_pos = lax.broadcasted_iota(jnp.int32, (seq, seq), 1)
    causal = row_pos >= col_pos

    def attention_part(i):
        slot = lax.rem(i, 2)
        gx = gather_x(i)
        xf[slot, rows_of(me, shard)] = xs[i]
        ln_shard(i, me)
        gx.near()
        ln_shard(i, left)
        ln_shard(i, right)
        gx.far()
        ln_shard(i, opp)
        for lo, hi in ((0, 768), (768, 1536), (1536, qkv_w)):
            got = jnp.dot(nb[...], wqkv[:, lo:hi], preferred_element_type=F32)
            qkv[:, lo:hi] = (got + bqkv_ref[:, lo:hi]).astype(BF16)
        outs = []
        for n in range(heads):
            at = 3 * head_dim * n
            q = qkv[:, at : at + head_dim]
            k = qkv[:, at + head_dim : at + 2 * head_dim]
            v = qkv[:, at + 2 * head_dim : at + 3 * head_dim]
            scores = lax.dot_general(q, k, (((1,), (1,)), ((), ())), preferred_element_type=F32) * head_dim**-0.5
            scores = jnp.where(causal, scores, -1e30)
            e = jnp.exp(scores - jnp.max(scores, axis=-1, keepdims=True))
            probs = (e / jnp.sum(e, axis=-1, keepdims=True)).astype(BF16)
            outs.append(jnp.dot(probs, v, preferred_element_type=F32).astype(BF16))
        cf[slot, me] = jnp.concatenate(outs, axis=-1)
        gather_c(i).start()

    chunk = 512
    n_chunks = width // chunk

    def over_columns(f):
        def body(n, c):
            f(pl.ds(pl.multiple_of(n * chunk, chunk), chunk))
            return c

        lax.fori_loop(0, n_chunks, body, 0)

    def out_block(i, owner, first):
        slot = lax.rem(i, 2)

        def f(cols):
            got = jnp.dot(cf[slot, owner], wout[rows_of(owner, own_k), cols], preferred_element_type=F32)
            acc[:, cols] = got if first else acc[:, cols] + got

        over_columns(f)

    def mlp_first(i):
        slot = lax.rem(i, 2)
        gc = gather_c(i)
        gc.near()
        out_block(i, left, False)
        out_block(i, right, False)
        gc.far()

        def f(cols):
            got = jnp.dot(cf[slot, opp], wout[rows_of(opp, own_k), cols], preferred_element_type=F32)
            a = (acc[:, cols] + got).astype(BF16).astype(F32)
            x1[:, cols] = (xf[slot, :, cols].astype(F32) + a + bout_ref[:, cols]).astype(BF16)

        over_columns(f)

        def ln2(r, c):
            at = rows_of(r, shard)
            nb[at] = norm_rows(x1[at], g2_ref[...], s2_ref[...])
            return c

        lax.fori_loop(0, ring, ln2, 0)

        def up(cols):
            got = jnp.dot(nb[...], wup[:, cols], preferred_element_type=F32) + bup_ref[:, cols]
            hid[:, cols] = jnp.maximum(got, 0.0).astype(BF16)

        over_columns(up)

    def mlp_second(i):
        slot = lax.rem(i, 2)

        def down(cols):
            part[slot, :, cols] = jnp.dot(hid[...], wdn[:, cols], preferred_element_type=F32).astype(BF16)

        over_columns(down)
        scatter_start(i)

    def remote_out(i):
        return (stage < last) | (i < per_stage * last)

    def next_copy(i):
        slot = lax.rem(i, 2)
        return pltpu.make_async_remote_copy(
            src_ref=x2.at[slot], dst_ref=xs.at[i], send_sem=pp_send.at[slot], recv_sem=xs_sem.at[i],
            device_id={"pp": lax.rem(stage + 1, num_stages)}, device_id_type=MESH,
        )

    def out_copy(i):
        slot = lax.rem(i, 2)
        at = lax.rem(i, per_stage)
        return pltpu.make_async_remote_copy(
            src_ref=x2.at[slot], dst_ref=obuf.at[at], send_sem=pp_send.at[slot], recv_sem=o_sem.at[at],
            device_id={"pp": i // per_stage}, device_id_type=MESH,
        )

    def hand_on(i):
        slot = lax.rem(i, 2)
        pl.when((i >= 2) & remote_out(i - 2))(lambda: next_copy(i).wait_send())
        sums = scatter_finish(i)
        own = rows_of(me, shard)
        for h in range(2):
            cols = pl.ds(h * half, half)
            m = sums[h].astype(BF16).astype(F32)
            x2[slot, :, cols] = (x1_own(i)[:, cols].astype(F32) + m + bdn_ref[:, cols]).astype(BF16)
        del own
        pl.when(stage < last)(lambda: next_copy(i).start())
        pl.when((stage == last) & (i < per_stage * last))(lambda: out_copy(i).start())

        @pl.when((stage == last) & (i >= per_stage * last))
        def _():
            obuf[lax.rem(i, per_stage)] = x2[slot]

    def x1_own(i):
        return x1.at[rows_of(me, shard)]

    def begin(i):
        x_arrival(i)
        gather_x(i).start()

    load_out.wait()
    pl.when(stage == 0)(lambda: begin(0))

    pl.when(lax.rem(stage, 2) == 1)(lambda: pl.semaphore_wait(turn_sem, 1))
    gather_w.start()
    gather_w.forward()
    gather_w.near()
    gather_w.far()
    pl.when(lax.rem(stage, 2) == 0)(
        lambda: pl.semaphore_signal(turn_sem, inc=1, device_id={"pp": stage + 1}, device_id_type=MESH)
    )
    load_qkv.wait()
    load_up.wait()
    load_dn.wait()

    pl.when(stage > 0)(lambda: begin(0))
    gather_x(0).forward()

    def step(i, carry):
        here = i < num_micro
        more = i < num_micro - 1
        pl.when(here)(lambda: attention_part(i))
        pl.when(here)(lambda: out_block(i, me, True))
        pl.when(i >= 1)(lambda: scatter_relay(i - 1))
        pl.when(i >= 1)(lambda: hand_on(i - 1))
        pl.when(here)(lambda: gather_c(i).forward())
        pl.when(more)(lambda: begin(i + 1))
        pl.when(here)(lambda: mlp_first(i))
        pl.when(more)(lambda: gather_x(i + 1).forward())
        pl.when(here)(lambda: mlp_second(i))
        return carry

    lax.fori_loop(0, num_micro + 1, step, 0)

    for i in range(num_micro - 2, num_micro):
        pl.when(stage < last)(lambda i=i: next_copy(i).wait_send())
        if i < per_stage * last:
            pl.when(stage == last)(lambda i=i: out_copy(i).wait_send())

    @pl.when(stage < last)
    def _():
        for j in range(per_stage):
            out_copy(j).wait_recv()

    out_ref[...] = obuf[...]


def solution(mesh):
    num_stages = mesh.shape["pp"]
    ring = mesh.shape["tp"]
    in_specs = (P("dp", None, "tp", None),
                P("pp", None), P("pp", None), P("pp", None, "tp"), P("pp", "tp"),
                P("pp", "tp", None, None), P("pp", None), P("pp", None), P("pp", None),
                P("pp", None, "tp"), P("pp", "tp"), P("pp", "tp", None), P("pp", None))
    out_specs = P(("dp", "pp"), None, "tp", None)

    def device_program(x_local, g1, s1, w_qkv, b_qkv, w_out, b_out, g2, s2, w_up, b_up, w_down, b_down):
        num_micro, batch, shard, width = x_local.shape
        local_heads, head_dim = w_out.shape[1], w_out.shape[2]
        own_k = local_heads * head_dim
        qkv_w, ff = w_qkv.shape[2], w_up.shape[2]
        rows = batch * shard
        seq = rows * ring
        half = width // 2
        per_stage = num_micro // num_stages
        hbm = pl.BlockSpec(memory_space=pl.ANY)
        vmem = pl.BlockSpec(memory_space=pltpu.VMEM)
        dma = pltpu.SemaphoreType.DMA
        out = pl.pallas_call(
            functools.partial(layer_kernel, num_stages, ring, head_dim),
            name="layers",
            out_shape=jax.ShapeDtypeStruct((per_stage, rows, width), BF16),
            in_specs=[hbm, vmem, vmem, hbm, vmem, hbm, vmem, vmem, vmem, hbm, vmem, hbm, vmem],
            out_specs=vmem,
            scratch_shapes=[
                pltpu.VMEM((width, qkv_w), BF16),
                pltpu.VMEM((own_k * ring, width), BF16),
                pltpu.VMEM((width, ff), BF16),
                pltpu.VMEM((ff, width), BF16),
                pltpu.VMEM((num_micro, rows, width), BF16),
                pltpu.VMEM((2, seq, width), BF16),
                pltpu.VMEM((seq, width), BF16),
                pltpu.VMEM((seq, qkv_w), BF16),
                pltpu.VMEM((2, ring, seq, own_k), BF16),
                pltpu.VMEM((seq, width), F32),
                pltpu.VMEM((seq, width), BF16),
                pltpu.VMEM((seq, ff), BF16),
                pltpu.VMEM((2, seq, width), BF16),
                pltpu.VMEM((2, 2, rows, half), BF16),
                pltpu.VMEM((2, 2, rows, half), BF16),
                pltpu.VMEM((2, 4, rows, half), BF16),
                pltpu.VMEM((2, rows, width), BF16),
                pltpu.VMEM((per_stage, rows, width), BF16),
                dma((4,)),
                dma((6,)),
                dma((6,)),
                dma((num_micro,)),
                dma((2, 6)),
                dma((2, 6)),
                dma((2, 6)),
                dma((2, 6)),
                dma((2, 6)),
                dma((2, 6)),
                dma((2,)),
                dma((per_stage,)),
                pltpu.SemaphoreType.REGULAR,
            ],
            compiler_params=pltpu.CompilerParams(
                collective_id=0, has_side_effects=True, vmem_limit_bytes=67_043_328
            ),
        )(
            x_local.reshape(num_micro, rows, width), g1, s1, w_qkv[0], b_qkv, w_out.reshape(own_k, width), b_out,
            g2, s2, w_up[0], b_up, w_down[0], b_down,
        )
        return out.reshape(per_stage, batch, shard, width)

    return jax.shard_map(device_program, mesh=mesh, in_specs=in_specs, out_specs=out_specs, check_vma=False)
```

time: 2430 us -> 846 us (0.35)
  waiting for transfers between devices: 1080 us -> 0 us
  Pallas kernels: 0 us -> 844 us
  matrix products: 558 us -> 0 us
  blocking collectives: 522 us -> 0 us
  other arithmetic: 129 us -> 0 us
  local copies, waits for them, and re-layouts: 71.5 us -> 1.72 us
  starting transfers between devices: 44.5 us -> 0 us
    reduce_scatter x46 -> x0, waiting for transfers between devices: 963 us -> none  [the longest x23 509 us: stage_layer(): lax.psum_scatter(attn_part, 'tp', scatter_dimension=1, tiled=True)]
    pallas_call x0 -> x1, Pallas kernels: none -> 844 us  [device_program(): pl.pallas_call(functools.partial(layer_kernel, num_stages, ring, head_dim...]
    all_gather x46 -> x0, blocking collectives: 522 us -> none  [the longest x23 272 us: stage_layer(): gathered_mid = lax.all_gather(normed_mid, 'tp', axis=1, tiled=True)]
    dot_general x69 -> x0, matrix products: 509 us -> none  [the longest x23 297 us: stage_layer(): jnp.einsum('bsf,fd->bsd', hidden, w_down, preferred_element_type=jnp.floa...]
    ppermute x30 -> x0, waiting for transfers between devices: 117 us -> none  [the longest x23 108 us: tick_body(): incoming = lax.ppermute(layer_out, 'pp', perm=send_next)]
    reduce_sum x92 -> x0, other arithmetic: 60 us -> none  [the longest x46 49.7 us: layer_norm(): row_mean = jnp.mean(rows_f32, axis=-1, keepdims=True)]
    sub x23 -> x0, matrix products: 49.4 us -> none  [causal_attention(): attn_probs = jax.nn.softmax(scores, axis=-1).astype(jnp.bfloat16)]
    convert_element_type x23 -> x0, local copies, waits for them, and re-layouts: 46.4 us -> none  [stage_layer(): (jnp.einsum('bsd,de->bse', gathered, w_qkv, preferred_element_type=jnp.fl...]
  transfers between devices with their start and end apart: 76 -> 0, of which waited for: 72 -> 0; matrix products, arithmetic and copies ran while one was open for 1% -> 0% of each run, Pallas kernels for 0% -> 0%
where the time goes in v1:
time: 846 us
  Pallas kernels  844 us (100%)
    pallas_call x1, Pallas kernels, device_program(): pl.pallas_call(functools.partial(layer_kernel, num_stages, ring, head_dim...  844 us

profile of v1, /device:TPU:103, one launch (start us, length us, event | category | flops | bytes accessed | tf_op | source)
XLA Modules:
  0.0 845.9 jit_solution(4095863651866984838)
XLA Ops:
  0.0 844.1 %layers.1 = bf16[2,32,2560]{2,1,0:T(8,128)(2,1)} custom-call(bf16[16,32,2560]{2,1,0:T(8,128)(2,1)} %bitcast.12, f32[1,2560]{1,0:T(1,128)} %g1_ref.1, f32[1,2560]{1,0:T(1,128)} %s1_ref.1, bf16[2560,1920]{1,0:T(8,128)(2,1)} %bitcast.10, f32[1,1920]{1,0:T(1,128)} %bqkv_ref.1, bf16[640,2560]{1,0:T(8,128)(2,1)} %bitcast.11, f32[1,2560]{1,0:T(1,128)} %bout_ref.1, ...), custom_call_target="tpu_custom_call" | custom-call | tf_op jit(solution)/shard_map/layers/pallas_call | solution.py:427
  844.1 1.7 copy.16

commit v2 on v1

v2 whole, which is shorter than its diff:
```python
import functools

import jax
import jax.numpy as jnp
from jax import lax
from jax.experimental import pallas as pl
from jax.experimental.pallas import tpu as pltpu
from jax.sharding import PartitionSpec as P

LN_EPS = 1e-5
MESH = pl.DeviceIdType.MESH
F32 = jnp.float32
BF16 = jnp.bfloat16


def norm_rows(rows, gain, shift):
    rows = rows.astype(F32)
    centered = rows - jnp.mean(rows, axis=-1, keepdims=True)
    var = jnp.mean(centered * centered, axis=-1, keepdims=True)
    return (centered * lax.rsqrt(var + LN_EPS) * gain + shift).astype(BF16)


def layer_kernel(
    num_stages, ring, head_dim,
    x_hbm, g1_ref, s1_ref, wqkv_hbm, bqkv_ref, wout_hbm, bout_ref,
    g2_ref, s2_ref, wup_hbm, bup_ref, wdn_hbm, bdn_ref,
    out_ref,
    wqkv, wout, wup, wdn,
    xf, nb, qkv, cf, acc, x1, hid, part, fin, x2, obuf,
    w_sem, wg_send, wg_recv, xb_send, xr_send, xr_recv, ac_send, ac_recv,
    rs_send, rs_recv, pp_send, o_sem, turn_sem, free_sem,
):
    num_micro, shard, width = x_hbm.shape
    seq = shard * ring
    per_stage = num_micro // num_stages
    own_k = wout_hbm.shape[0]
    qkv_w = wqkv_hbm.shape[1]
    heads = own_k // head_dim
    half = width // 2
    last = num_stages - 1
    depth = xf.shape[0]

    me = lax.axis_index("tp")
    stage = lax.axis_index("pp")
    right = lax.rem(me + 1, ring)
    left = lax.rem(me + ring - 1, ring)
    opp = lax.rem(me + 2, ring)
    to_right, to_left, to_opp = {"tp": right}, {"tp": left}, {"tp": opp}

    def rows_of(owner, n):
        return pl.ds(pl.multiple_of(owner * n, n), n)

    def remote(src, dst, send, recv, device):
        return pltpu.make_async_remote_copy(
            src_ref=src, dst_ref=dst, send_sem=send, recv_sem=recv, device_id=device, device_id_type=MESH
        )

    def signal(sem, device):
        pl.semaphore_signal(sem, inc=1, device_id=device, device_id_type=MESH)

    barrier = pltpu.get_barrier_semaphore()

    def beside(pp):
        return ({"pp": pp}, {"tp": right, "pp": pp}, {"tp": left, "pp": pp})

    for device in (to_right, to_left, to_opp):
        signal(barrier, device)

    @pl.when(stage > 0)
    def _():
        for device in beside(stage - 1):
            signal(barrier, device)

    @pl.when(stage < last)
    def _():
        for device in beside(stage + 1):
            signal(barrier, device)

    pl.when(stage < last - 1)(lambda: signal(barrier, {"pp": last}))

    @pl.when(stage == last)
    def _():
        for q in range(last - 1):
            signal(barrier, {"pp": q})

    load_out = pltpu.make_async_copy(wout_hbm, wout.at[rows_of(me, own_k)], w_sem.at[0])
    load_qkv = pltpu.make_async_copy(wqkv_hbm, wqkv, w_sem.at[1])
    load_up = pltpu.make_async_copy(wup_hbm, wup, w_sem.at[2])
    load_dn = pltpu.make_async_copy(wdn_hbm, wdn, w_sem.at[3])
    load_out.start()
    load_qkv.start()
    load_up.start()
    load_dn.start()

    pl.semaphore_wait(
        barrier,
        3
        + jnp.where(stage > 0, 3, 0)
        + jnp.where(stage < last, 3, 0)
        + jnp.where(stage < last - 1, 1, 0)
        + jnp.where(stage == last, last - 1, 0),
    )

    class Gather:
        def __init__(self, piece, send, recv):
            self.piece, self.send, self.recv = piece, send, recv

        def copy(self, k, owner, h, device):
            return remote(self.piece(owner, h), self.piece(owner, h), self.send.at[k], self.recv.at[k], device)

        def hop1(self):
            return (
                self.copy(0, me, 0, to_right),
                self.copy(3, me, 1, to_left),
                self.copy(1, me, 1, to_right),
                self.copy(2, me, 0, to_left),
            )

        def fwd(self):
            return self.copy(4, left, 0, to_right), self.copy(5, right, 1, to_left)

        def start(self):
            for c in self.hop1():
                c.start()

        def recv_wait(self, k, owner, h):
            self.copy(k, owner, h, to_right).wait_recv()

        def forward(self):
            a, b = self.fwd()
            self.recv_wait(0, left, 0)
            a.start()
            self.recv_wait(3, right, 1)
            b.start()

        def near(self):
            self.recv_wait(1, left, 1)
            self.recv_wait(2, right, 0)

        def far(self):
            self.recv_wait(4, opp, 0)
            self.recv_wait(5, opp, 1)
            for c in self.fwd():
                c.wait_send()

        def sent(self):
            for c in self.hop1():
                c.wait_send()

    wk = own_k // 2
    gather_w = Gather(
        lambda owner, h: wout.at[pl.ds(pl.multiple_of(owner * own_k + h * wk, wk), wk)], wg_send, wg_recv
    )

    def gather_c(i):
        slot = lax.rem(i, 2)
        ch = seq // 2
        return Gather(lambda owner, h: cf.at[slot, owner, pl.ds(h * ch, ch)], ac_send.at[slot], ac_recv.at[slot])

    xh = shard // 2

    def gather_x(i):
        slot = lax.rem(i, depth)

        def piece(owner, h):
            return xf.at[slot, pl.ds(pl.multiple_of(owner * shard + h * xh, xh), xh)]

        return Gather(piece, xr_send.at[slot], xr_recv.at[slot])

    def x_own(i, src):
        slot = lax.rem(i, depth)
        return pltpu.make_async_copy(src, xf.at[slot, rows_of(me, shard)], xr_recv.at[slot, 6])

    def x_copies(i, src, send, pp):
        g = gather_x(i)

        def copy(k, h, tp):
            return remote(src(h), g.piece(me, h), send.at[k], g.recv.at[k], {"tp": tp, "pp": pp})

        return copy(0, 0, right), copy(3, 1, left), copy(1, 1, right), copy(2, 0, left)

    def begin_copies(i):
        return x_copies(i, lambda h: x_hbm.at[i, pl.ds(h * xh, xh)], xb_send.at[lax.rem(i, depth)], stage)

    def begin(i):
        for c in begin_copies(i):
            c.start()
        x_own(i, x_hbm.at[i]).start()

    def scatter(i, c):
        slot = lax.rem(i, 2)
        cols = pl.ds(c * half, half)

        def copy(k, owner, device):
            return remote(
                part.at[slot, rows_of(owner, shard), cols], fin.at[slot, k, :, cols],
                rs_send.at[slot, c, k], rs_recv.at[slot, c, k], device,
            )

        return copy(2, opp, to_opp), copy(0, right, to_right), copy(1, left, to_left)

    def ln_shard(i, owner):
        at = rows_of(owner, shard)
        nb[at] = norm_rows(xf[lax.rem(i, depth), at], g1_ref[...], s1_ref[...])

    causal = lax.broadcasted_iota(jnp.int32, (seq, seq), 0) >= lax.broadcasted_iota(jnp.int32, (seq, seq), 1)

    def attention_part(i):
        slot = lax.rem(i, 2)
        gx = gather_x(i)
        x_own(i, x_hbm.at[i]).wait()
        ln_shard(i, me)
        gx.near()
        ln_shard(i, left)
        ln_shard(i, right)
        gx.far()

        @pl.when(stage == 0)
        def _():
            for c in begin_copies(i):
                c.wait_send()

        ln_shard(i, opp)
        for lo, hi in ((0, 768), (768, 1536), (1536, qkv_w)):
            got = jnp.dot(nb[...], wqkv[:, lo:hi], preferred_element_type=F32)
            qkv[:, lo:hi] = (got + bqkv_ref[:, lo:hi]).astype(BF16)

        def part_of(n, j):
            at = (3 * n + j) * head_dim
            return qkv[:, at : at + head_dim]

        scores = [
            lax.dot_general(part_of(n, 0), part_of(n, 1), (((1,), (1,)), ((), ())), preferred_element_type=F32)
            for n in range(heads)
        ]
        probs = []
        for s in scores:
            s = jnp.where(causal, s * head_dim**-0.5, -1e30)
            e = jnp.exp(s - jnp.max(s, axis=-1, keepdims=True))
            probs.append((e * (1.0 / jnp.sum(e, axis=-1, keepdims=True))).astype(BF16))
        outs = [jnp.dot(p, part_of(n, 2), preferred_element_type=F32).astype(BF16) for n, p in enumerate(probs)]
        cf[slot, me] = jnp.concatenate(outs, axis=-1)
        gather_c(i).start()

    chunk = 512

    def out_block(i, owner, cols):
        return jnp.dot(cf[lax.rem(i, 2), owner], wout[rows_of(owner, own_k), cols], preferred_element_type=F32)

    def over_columns(f, lo=0, hi=width):
        for at in range(lo, hi, chunk):
            f(pl.ds(at, min(chunk, hi - at)))

    def out_own(i):
        def f(cols):
            acc[:, cols] = out_block(i, me, cols)

        over_columns(f)

    def mlp_first(i):
        slot = lax.rem(i, depth)
        gc = gather_c(i)
        gc.near()

        def near(cols):
            acc[:, cols] = acc[:, cols] + out_block(i, left, cols) + out_block(i, right, cols)

        over_columns(near)
        gc.far()

        def far(cols):
            a = (acc[:, cols] + out_block(i, opp, cols)).astype(BF16).astype(F32)
            x1[:, cols] = (xf[slot, :, cols].astype(F32) + a + bout_ref[:, cols]).astype(BF16)

        over_columns(far)
        gc.sent()

        @pl.when((stage > 0) & (i < num_micro - depth))
        def _():
            for k, device in zip((0, 2, 1), beside(stage - 1)):
                signal(free_sem.at[k], device)

        for r in range(ring):
            at = pl.ds(r * shard, shard)
            nb[at] = norm_rows(x1[at], g2_ref[...], s2_ref[...])

        def up(cols):
            got = jnp.dot(nb[...], wup[:, cols], preferred_element_type=F32) + bup_ref[:, cols]
            hid[:, cols] = jnp.maximum(got, 0.0).astype(BF16)

        over_columns(up)

    def mlp_second(i):
        slot = lax.rem(i, 2)

        def down(cols):
            part[slot, :, cols] = jnp.dot(hid[...], wdn[:, cols], preferred_element_type=F32).astype(BF16)

        for c in range(2):
            over_columns(down, c * half, (c + 1) * half)
            for copy in scatter(i, c):
                copy.start()

    def next_copies(i):
        slot = lax.rem(i, 2)
        send = pp_send.at[slot]
        pp = lax.rem(stage + 1, num_stages)
        own = remote(
            x2.at[slot], xf.at[lax.rem(i, depth), rows_of(me, shard)], send.at[4],
            xr_recv.at[lax.rem(i, depth), 6], {"pp": pp},
        )
        return *x_copies(i, lambda h: x2.at[slot, pl.ds(h * xh, xh)], send, pp), own

    def out_copy(i):
        slot = lax.rem(i, 2)
        at = lax.rem(i, per_stage)
        return remote(x2.at[slot], obuf.at[at], pp_send.at[slot, 4], o_sem.at[at], {"pp": i // per_stage})

    def sent_on(i):
        @pl.when(stage < last)
        def _():
            for c in next_copies(i):
                c.wait_send()

        pl.when((stage == last) & (i < per_stage * last))(lambda: out_copy(i).wait_send())

    def hand_on(i):
        slot = lax.rem(i, 2)
        pl.when(i >= 2)(lambda: sent_on(i - 2))
        own = rows_of(me, shard)
        for c in range(2):
            copies = scatter(i, c)
            for copy in copies:
                copy.wait_recv()
            cols = pl.ds(c * half, half)
            m = part[slot, own, cols].astype(F32)
            for k in range(3):
                m = m + fin[slot, k, :, cols].astype(F32)
            m = m.astype(BF16).astype(F32)
            x2[slot, :, cols] = (x1[own, cols].astype(F32) + m + bdn_ref[:, cols]).astype(BF16)

        @pl.when(stage < last)
        def _():
            @pl.when(i >= depth)
            def _():
                for k in range(3):
                    pl.semaphore_wait(free_sem.at[k], 1)

            for c in next_copies(i):
                c.start()

        pl.when((stage == last) & (i < per_stage * last))(lambda: out_copy(i).start())

        @pl.when((stage == last) & (i >= per_stage * last))
        def _():
            obuf[lax.rem(i, per_stage)] = x2[slot]

        for c in range(2):
            for copy in scatter(i, c):
                copy.wait_send()

    @pl.when(stage == 0)
    def _():
        begin(0)
        begin(1)

    load_out.wait()

    pl.when(lax.rem(stage, 2) == 1)(lambda: pl.semaphore_wait(turn_sem, 1))
    gather_w.start()
    gather_w.forward()
    gather_w.near()
    gather_w.far()
    gather_w.sent()
    pl.when(lax.rem(stage, 2) == 0)(lambda: signal(turn_sem, {"pp": stage + 1}))
    load_qkv.wait()
    load_up.wait()
    load_dn.wait()
    gather_x(0).forward()

    def step(i, carry):
        here = i < num_micro

        @pl.when(here)
        def _():
            attention_part(i)
            out_own(i)

        pl.when(i >= 1)(lambda: hand_on(i - 1))
        pl.when(here)(lambda: gather_c(i).forward())
        pl.when((stage == 0) & (i < num_micro - 2))(lambda: begin(i + 2))
        pl.when(here)(lambda: mlp_first(i))
        pl.when(i < num_micro - 1)(lambda: gather_x(i + 1).forward())
        pl.when(here)(lambda: mlp_second(i))
        return carry

    lax.fori_loop(0, num_micro + 1, step, 0)

    for i in range(num_micro - 2, num_micro):
        sent_on(i)

    @pl.when(stage < last)
    def _():
        for j in range(per_stage):
            out_copy(j).wait_recv()

    out_ref[...] = obuf[...]


def solution(mesh):
    num_stages = mesh.shape["pp"]
    ring = mesh.shape["tp"]
    in_specs = (P("dp", None, "tp", None),
                P("pp", None), P("pp", None), P("pp", None, "tp"), P("pp", "tp"),
                P("pp", "tp", None, None), P("pp", None), P("pp", None), P("pp", None),
                P("pp", None, "tp"), P("pp", "tp"), P("pp", "tp", None), P("pp", None))
    out_specs = P(("dp", "pp"), None, "tp", None)

    def device_program(x_local, g1, s1, w_qkv, b_qkv, w_out, b_out, g2, s2, w_up, b_up, w_down, b_down):
        num_micro, batch, shard, width = x_local.shape
        local_heads, head_dim = w_out.shape[1], w_out.shape[2]
        own_k = local_heads * head_dim
        qkv_w, ff = w_qkv.shape[2], w_up.shape[2]
        rows = batch * shard
        seq = rows * ring
        per_stage = num_micro // num_stages
        hbm = pl.BlockSpec(memory_space=pl.ANY)
        vmem = pl.BlockSpec(memory_space=pltpu.VMEM)
        dma = pltpu.SemaphoreType.DMA
        out = pl.pallas_call(
            functools.partial(layer_kernel, num_stages, ring, head_dim),
            name="layers",
            out_shape=jax.ShapeDtypeStruct((per_stage, rows, width), BF16),
            in_specs=[hbm, vmem, vmem, hbm, vmem, hbm, vmem, vmem, vmem, hbm, vmem, hbm, vmem],
            out_specs=vmem,
            scratch_shapes=[
                pltpu.VMEM((width, qkv_w), BF16),
                pltpu.VMEM((own_k * ring, width), BF16),
                pltpu.VMEM((width, ff), BF16),
                pltpu.VMEM((ff, width), BF16),
                pltpu.VMEM((4, seq, width), BF16),
                pltpu.VMEM((seq, width), BF16),
                pltpu.VMEM((seq, qkv_w), BF16),
                pltpu.VMEM((2, ring, seq, own_k), BF16),
                pltpu.VMEM((seq, width), F32),
                pltpu.VMEM((seq, width), BF16),
                pltpu.VMEM((seq, ff), BF16),
                pltpu.VMEM((2, seq, width), BF16),
                pltpu.VMEM((2, 3, rows, width), BF16),
                pltpu.VMEM((2, rows, width), BF16),
                pltpu.VMEM((per_stage, rows, width), BF16),
                dma((4,)),
                dma((6,)),
                dma((6,)),
                dma((4, 4)),
                dma((4, 6)),
                dma((4, 7)),
                dma((2, 6)),
                dma((2, 6)),
                dma((2, 2, 3)),
                dma((2, 2, 3)),
                dma((2, 5)),
                dma((per_stage,)),
                pltpu.SemaphoreType.REGULAR,
                pltpu.SemaphoreType.REGULAR((3,)),
            ],
            compiler_params=pltpu.CompilerParams(
                collective_id=0, has_side_effects=True, vmem_limit_bytes=67_043_328
            ),
        )(
            x_local.reshape(num_micro, rows, width), g1, s1, w_qkv[0], b_qkv, w_out.reshape(own_k, width), b_out,
            g2, s2, w_up[0], b_up, w_down[0], b_down,
        )
        return out.reshape(per_stage, batch, shard, width)

    return jax.shard_map(device_program, mesh=mesh, in_specs=in_specs, out_specs=out_specs, check_vma=False)
```

time: 846 us -> 700 us (0.83)
  Pallas kernels: 844 us -> 698 us
    pallas_call x1, Pallas kernels: 844 us -> 698 us  [device_program(): pl.pallas_call(functools.partial(layer_kernel, num_stages, ring, head_dim...]
where the time goes in v2:
time: 700 us
  Pallas kernels  698 us (100%)
    pallas_call x1, Pallas kernels, device_program(): pl.pallas_call(functools.partial(layer_kernel, num_stages, ring, head_dim...  698 us

profile of v2, /device:TPU:103, one launch (start us, length us, event | category | flops | bytes accessed | tf_op | source)
XLA Modules:
  0.0 699.9 jit_solution(12904906265759421433)
XLA Ops:
  0.0 698.1 %layers.1 = bf16[2,32,2560]{2,1,0:T(8,128)(2,1)} custom-call(bf16[16,32,2560]{2,1,0:T(8,128)(2,1)} %bitcast.12, f32[1,2560]{1,0:T(1,128)} %g1_ref.1, f32[1,2560]{1,0:T(1,128)} %s1_ref.1, bf16[2560,1920]{1,0:T(8,128)(2,1)} %bitcast.10, f32[1,1920]{1,0:T(1,128)} %bqkv_ref.1, bf16[640,2560]{1,0:T(8,128)(2,1)} %bitcast.11, f32[1,2560]{1,0:T(1,128)} %bout_ref.1, ...), custom_call_target="tpu_custom_call" | custom-call | tf_op jit(solution)/shard_map/layers/pallas_call | solution.py:430
  698.2 1.7 copy.16

commit v3 on v2

--- a/solution.py
+++ b/solution.py
@@ -9,6 +9,9 @@
 
 LN_EPS = 1e-5
 MESH = pl.DeviceIdType.MESH
+PARTS = 2
+CUT_FIFTHS = (2, 2, 1)
+POINTS = {"H0": 2, "He": 2, "Ho": 2, "F0": 5, "Fe": 5, "Fo": 6, "f0": 6, "fe": 6, "fo": 6}
 F32 = jnp.float32
 BF16 = jnp.bfloat16
 
@@ -27,8 +30,8 @@
     out_ref,
     wqkv, wout, wup, wdn,
     xf, nb, qkv, cf, acc, x1, hid, part, fin, x2, obuf,
-    w_sem, wg_send, wg_recv, xb_send, xr_send, xr_recv, ac_send, ac_recv,
-    rs_send, rs_recv, pp_send, o_sem, turn_sem, free_sem,
+    w_sem, wg_send, wg_recv, wh_send, wh_recv, wx_send, wx_recv, wr_send, wr_recv, xb_send, xr_send, xr_recv, ac_send, ac_recv,
+    rs_send, rs_recv, st_send, pp_send, o_sem, turn_sem, free_sem,
 ):
     num_micro, shard, width = x_hbm.shape
     seq = shard * ring
@@ -36,7 +39,8 @@
     own_k = wout_hbm.shape[0]
     qkv_w = wqkv_hbm.shape[1]
     heads = own_k // head_dim
-    half = width // 2
+    fifth = width // 5
+    cuts = tuple(pl.ds(sum(CUT_FIFTHS[:c]) * fifth, n * fifth) for c, n in enumerate(CUT_FIFTHS))
     last = num_stages - 1
     depth = xf.shape[0]
 
@@ -58,6 +62,17 @@
     def signal(sem, device):
         pl.semaphore_signal(sem, inc=1, device_id=device, device_id_type=MESH)
 
+    lends = (stage < 2) | (stage == 3)
+
+    def helper(p):
+        return stage + (jnp.where(stage == 3, 2, last - 1), 2)[p]
+
+    def helped(p):
+        return stage - (jnp.where(stage == 5, 2, last - 1), 2)[p]
+
+    def helps(p):
+        return ((stage >= last - 1) | (stage == 5), (stage == 2) | (stage == 3) | (stage == 5))[p]
+
     barrier = pltpu.get_barrier_semaphore()
 
     def beside(pp):
@@ -77,6 +92,17 @@
             signal(barrier, device)
 
     pl.when(stage < last - 1)(lambda: signal(barrier, {"pp": last}))
+
+    for here, there in ((0, 1), (1, 0)):
+        pl.when(stage == here)(lambda there=there: signal(barrier, {"tp": opp, "pp": there}))
+
+    @pl.when(lends)
+    def _():
+        for p in range(2):
+            signal(barrier, {"pp": helper(p)})
+
+    pl.when(helps(0))(lambda: signal(barrier, {"pp": helped(0)}))
+    pl.when(helps(1))(lambda: signal(barrier, {"pp": helped(1)}))
 
     @pl.when(stage == last)
     def _():
@@ -90,7 +116,7 @@
     load_out.start()
     load_qkv.start()
     load_up.start()
-    load_dn.start()
+    pl.when(~(helps(0) | helps(1)))(load_dn.start)
 
     pl.semaphore_wait(
         barrier,
@@ -98,89 +124,220 @@
         + jnp.where(stage > 0, 3, 0)
         + jnp.where(stage < last, 3, 0)
         + jnp.where(stage < last - 1, 1, 0)
-        + jnp.where(stage == last, last - 1, 0),
+        + jnp.where(stage == last, last - 1, 0)
+        + jnp.where(stage < 2, 1, 0)
+        + jnp.where(lends, 2, 0)
+        + jnp.where(helps(0), 1, 0)
+        + jnp.where(helps(1), 1, 0),
     )
 
     class Gather:
-        def __init__(self, piece, send, recv):
-            self.piece, self.send, self.recv = piece, send, recv
-
-        def copy(self, k, owner, h, device):
-            return remote(self.piece(owner, h), self.piece(owner, h), self.send.at[k], self.recv.at[k], device)
+        def __init__(self, piece, send, recv, parts=PARTS):
+            self.piece, self.send, self.recv, self.parts = piece, send, recv, parts
+            self.straight = None
+
+        def copy(self, k, src, dst, device):
+            return remote(src, dst, self.send.at[k], self.recv.at[k], device)
+
+        def near_copies(self, src, right_device, left_device):
+            n = self.parts
+            first = []
+            for j in range(n):
+                first.append(self.copy(j, src(0, j), self.piece(me, 0, j), right_device))
+                first.append(self.copy(n + j, src(1, j), self.piece(me, 1, j), left_device))
+            return (
+                *first,
+                self.copy(2 * n, src(1, None), self.piece(me, 1, None), right_device),
+                self.copy(2 * n + 1, src(0, None), self.piece(me, 0, None), left_device),
+            )
 
         def hop1(self):
-            return (
-                self.copy(0, me, 0, to_right),
-                self.copy(3, me, 1, to_left),
-                self.copy(1, me, 1, to_right),
-                self.copy(2, me, 0, to_left),
-            )
+            return self.near_copies(lambda h, j: self.piece(me, h, j), to_right, to_left)
 
         def fwd(self):
-            return self.copy(4, left, 0, to_right), self.copy(5, right, 1, to_left)
+            n = self.parts
+            pairs = []
+            for j in range(n):
+                pairs.append((j, self.copy(2 * n + 2 + j, self.piece(left, 0, j), self.piece(left, 0, j), to_right)))
+                pairs.append((n + j, self.copy(3 * n + 2 + j, self.piece(right, 1, j), self.piece(right, 1, j), to_left)))
+            return pairs
 
         def start(self):
             for c in self.hop1():
                 c.start()
 
-        def recv_wait(self, k, owner, h):
-            self.copy(k, owner, h, to_right).wait_recv()
+        def arrived(self, k, owner, h, j):
+            self.copy(k, self.piece(owner, h, j), self.piece(owner, h, j), to_right).wait_recv()
 
         def forward(self):
-            a, b = self.fwd()
-            self.recv_wait(0, left, 0)
-            a.start()
-            self.recv_wait(3, right, 1)
-            b.start()
+            n = self.parts
+            for k, c in self.fwd():
+                self.arrived(k, *((left, 0, k) if k < n else (right, 1, k - n)))
+                c.start() if self.straight is None else pl.when(~self.straight)(c.start)
 
         def near(self):
-            self.recv_wait(1, left, 1)
-            self.recv_wait(2, right, 0)
+            n = self.parts
+            self.arrived(2 * n, left, 1, None)
+            self.arrived(2 * n + 1, right, 0, None)
 
         def far(self):
-            self.recv_wait(4, opp, 0)
-            self.recv_wait(5, opp, 1)
-            for c in self.fwd():
-                c.wait_send()
+            n = self.parts
+            for j in range(n):
+                self.arrived(2 * n + 2 + j, opp, 0, j)
+                self.arrived(3 * n + 2 + j, opp, 1, j)
+
+            def forwarded():
+                for _, c in self.fwd():
+                    c.wait_send()
+
+            forwarded() if self.straight is None else pl.when(~self.straight)(forwarded)
 
         def sent(self):
             for c in self.hop1():
                 c.wait_send()
 
-    wk = own_k // 2
-    gather_w = Gather(
-        lambda owner, h: wout.at[pl.ds(pl.multiple_of(owner * own_k + h * wk, wk), wk)], wg_send, wg_recv
-    )
+        def finish(self):
+            self.near()
+            self.far()
+            self.sent()
+
+    class Whole:
+        def __init__(self, by_y, by_x):
+            self.by_y, self.by_x = by_y, by_x
+            self.first = Gather(self.piece(0, by_y), wg_send.at[0], wg_recv.at[0], 1)
+            self.rest = Gather(self.piece(by_y, 2 * by_x), wg_send.at[1], wg_recv.at[1], 1)
+
+        @staticmethod
+        def half_of(n, h):
+            first = -(-n // 32) * 16
+            return (0, first) if h == 0 else (first, n - first)
+
+        def piece(self, lo, n):
+            def of(owner, h, j=None):
+                at, size = self.half_of(n, h)
+                return wout.at[pl.ds(pl.multiple_of(owner * own_k + lo + at, 16), size)]
+
+            return of
+
+        def path(self, p):
+            return self.piece(self.by_y + p * self.by_x, self.by_x)
+
+        def lent(self, p):
+            def of(owner, h, j=None):
+                at, size = self.half_of(self.by_x, h)
+                return wdn.at[pl.ds(pl.multiple_of((p * ring + owner) * self.by_x + at, 16), size)]
+
+            return of
+
+        def lend(self, p, h, pp):
+            return remote(self.path(p)(me, h), self.lent(p)(me, h), wx_send.at[p, h], wx_recv.at[p, h], {"pp": pp})
+
+        def give_back(self, p, k, pp):
+            owner, h = others[k]
+            return remote(
+                self.lent(p)(owner, h), self.path(p)(owner, h), wr_send.at[p, k], wr_recv.at[p, k], {"pp": pp}
+            )
+
+        def helper_ring(self, p):
+            return Gather(self.lent(p), wh_send.at[p], wh_recv.at[p], 1)
+
+        def help_gather(self, p, now):
+            pp, g = helped(p), self.helper_ring(p)
+            for h in range(2):
+                self.lend(p, h, pp).wait_recv()
+                for c in (g.hop1()[0], g.hop1()[3]) if h == 0 else (g.hop1()[1], g.hop1()[2]):
+                    c.start()
+            for k in range(6):
+                g.arrived(k, *others[k], None)
+                if k < 2:
+                    g.fwd()[k][1].start()
+                if now:
+                    self.give_back(p, k, pp).start()
+            if not now:
+                pl.semaphore_wait(turn_sem.at[2], 1)
+                for k in range(6):
+                    self.give_back(p, k, pp).start()
+
+        def help_end(self, p):
+            g = self.helper_ring(p)
+            g.sent()
+            for _, c in g.fwd():
+                c.wait_send()
+            for k in range(6):
+                self.give_back(p, k, helped(p)).wait_send()
+
+        def lend_all(self):
+            for h in range(2):
+                for p in range(2):
+                    self.lend(p, h, helper(p)).start()
+
+        def lent_all(self):
+            for h in range(2):
+                for p in range(2):
+                    self.lend(p, h, helper(p)).wait_send()
+
+        def end(self):
+            self.first.finish()
+            pl.when(stage == 0)(lambda: signal(turn_sem.at[0], {"pp": stage + 1}))
+            for p in range(2):
+                for k in range(6):
+                    self.give_back(p, k, helper(p)).wait_recv()
+
+    others = ((left, 0), (right, 1), (left, 1), (right, 0), (opp, 0), (opp, 1))
+    whole_even = Whole(own_k // 2, own_k // 4)
+    whole_odd = Whole(own_k // 2, own_k // 4)
 
     def gather_c(i):
         slot = lax.rem(i, 2)
         ch = seq // 2
-        return Gather(lambda owner, h: cf.at[slot, owner, pl.ds(h * ch, ch)], ac_send.at[slot], ac_recv.at[slot])
+        cn = ch // PARTS
+
+        def piece(owner, h, j=None):
+            rows = pl.ds(h * ch, ch) if j is None else pl.ds(h * ch + j * cn, cn)
+            return cf.at[slot, owner, rows]
+
+        return Gather(piece, ac_send.at[slot], ac_recv.at[slot])
 
     xh = shard // 2
+
+    xn = width // PARTS
+
+    def x_part(ref, h, j):
+        at = pl.ds(h * xh, xh)
+        return ref.at[at] if j is None else ref.at[at, pl.ds(j * xn, xn)]
 
     def gather_x(i):
         slot = lax.rem(i, depth)
 
-        def piece(owner, h):
-            return xf.at[slot, pl.ds(pl.multiple_of(owner * shard + h * xh, xh), xh)]
-
-        return Gather(piece, xr_send.at[slot], xr_recv.at[slot])
+        def piece(owner, h, j=None):
+            at = pl.ds(pl.multiple_of(owner * shard + h * xh, xh), xh)
+            return xf.at[slot, at] if j is None else xf.at[slot, at, pl.ds(j * xn, xn)]
+
+        g = Gather(piece, xr_send.at[slot], xr_recv.at[slot])
+        g.straight = (stage == 1) & (i == 0)
+        return g
 
     def x_own(i, src):
         slot = lax.rem(i, depth)
-        return pltpu.make_async_copy(src, xf.at[slot, rows_of(me, shard)], xr_recv.at[slot, 6])
-
-    def x_copies(i, src, send, pp):
+        return pltpu.make_async_copy(src, xf.at[slot, rows_of(me, shard)], xr_recv.at[slot, 4 * PARTS + 2])
+
+    def x_copies(i, ref, send, pp):
         g = gather_x(i)
-
-        def copy(k, h, tp):
-            return remote(src(h), g.piece(me, h), send.at[k], g.recv.at[k], {"tp": tp, "pp": pp})
-
-        return copy(0, 0, right), copy(3, 1, left), copy(1, 1, right), copy(2, 0, left)
+        g.send = send
+        return g.near_copies(lambda h, j: x_part(ref, h, j), {"tp": right, "pp": pp}, {"tp": left, "pp": pp})
+
+    def straight_copies():
+        g = gather_x(0)
+        n = g.parts
+        pp = {"tp": opp, "pp": lax.rem(stage + 1, num_stages)}
+        return [
+            remote(x_part(x2.at[0], h, j), g.piece(me, h, j), st_send.at[h * n + j], g.recv.at[(2 + h) * n + 2 + j], pp)
+            for j in range(n)
+            for h in range(2)
+        ]
 
     def begin_copies(i):
-        return x_copies(i, lambda h: x_hbm.at[i, pl.ds(h * xh, xh)], xb_send.at[lax.rem(i, depth)], stage)
+        return x_copies(i, x_hbm.at[i], xb_send.at[lax.rem(i, depth)], stage)
 
     def begin(i):
         for c in begin_copies(i):
@@ -189,7 +346,7 @@
 
     def scatter(i, c):
         slot = lax.rem(i, 2)
-        cols = pl.ds(c * half, half)
+        cols = cuts[c]
 
         def copy(k, owner, device):
             return remote(
@@ -204,6 +361,28 @@
         nb[at] = norm_rows(xf[lax.rem(i, depth), at], g1_ref[...], s1_ref[...])
 
     causal = lax.broadcasted_iota(jnp.int32, (seq, seq), 0) >= lax.broadcasted_iota(jnp.int32, (seq, seq), 1)
+
+    def slot_at(s, i):
+        even = lax.rem(stage, 2) == 0
+        kinds = {"0": stage == 0, "e": even & (stage > 0), "o": ~even}
+
+        def any_of(letter):
+            found = [kinds[k] for k in kinds if POINTS[letter + k] == s]
+            return functools.reduce(jnp.logical_or, found) if found else None
+
+        h, f, f_first = any_of("H"), any_of("F"), any_of("f")
+        if h is not None:
+            pl.when(h & (i >= 1))(lambda: hand_on(i - 1))
+        go = None
+        if f is not None:
+            go = f & (i > 0)
+        if f_first is not None:
+            g = f_first & (i == 0)
+            go = g if go is None else go | g
+        if go is not None:
+            pl.when(go & (i < num_micro - 1))(lambda: gather_x(i + 1).forward())
+        if s == 3:
+            pl.when((stage == 0) & (i < num_micro - 2))(lambda: begin(i + 2))
 
     def attention_part(i):
         slot = lax.rem(i, 2)
@@ -224,6 +403,7 @@
         for lo, hi in ((0, 768), (768, 1536), (1536, qkv_w)):
             got = jnp.dot(nb[...], wqkv[:, lo:hi], preferred_element_type=F32)
             qkv[:, lo:hi] = (got + bqkv_ref[:, lo:hi]).astype(BF16)
+        slot_at(1, i)
 
         def part_of(n, j):
             at = (3 * n + j) * head_dim
@@ -260,12 +440,15 @@
     def mlp_first(i):
         slot = lax.rem(i, depth)
         gc = gather_c(i)
+        pl.when((stage == 0) & (i == 0))(whole_even.end)
+        pl.when((stage == 1) & (i == 0))(whole_odd.end)
         gc.near()
 
         def near(cols):
             acc[:, cols] = acc[:, cols] + out_block(i, left, cols) + out_block(i, right, cols)
 
         over_columns(near)
+        slot_at(4, i)
         gc.far()
 
         def far(cols):
@@ -274,6 +457,7 @@
 
         over_columns(far)
         gc.sent()
+        slot_at(5, i)
 
         @pl.when((stage > 0) & (i < num_micro - depth))
         def _():
@@ -296,31 +480,38 @@
         def down(cols):
             part[slot, :, cols] = jnp.dot(hid[...], wdn[:, cols], preferred_element_type=F32).astype(BF16)
 
-        for c in range(2):
-            over_columns(down, c * half, (c + 1) * half)
+        for c in range(len(cuts)):
+            over_columns(down, cuts[c].start, cuts[c].start + cuts[c].size)
             for copy in scatter(i, c):
                 copy.start()
+            if c == 0:
+                slot_at(7, i)
 
     def next_copies(i):
         slot = lax.rem(i, 2)
         send = pp_send.at[slot]
         pp = lax.rem(stage + 1, num_stages)
         own = remote(
-            x2.at[slot], xf.at[lax.rem(i, depth), rows_of(me, shard)], send.at[4],
-            xr_recv.at[lax.rem(i, depth), 6], {"pp": pp},
+            x2.at[slot], xf.at[lax.rem(i, depth), rows_of(me, shard)], send.at[2 * PARTS + 2],
+            xr_recv.at[lax.rem(i, depth), 4 * PARTS + 2], {"pp": pp},
         )
-        return *x_copies(i, lambda h: x2.at[slot, pl.ds(h * xh, xh)], send, pp), own
+        return *x_copies(i, x2.at[slot], send, pp), own
 
     def out_copy(i):
         slot = lax.rem(i, 2)
         at = lax.rem(i, per_stage)
-        return remote(x2.at[slot], obuf.at[at], pp_send.at[slot, 4], o_sem.at[at], {"pp": i // per_stage})
+        return remote(x2.at[slot], obuf.at[at], pp_send.at[slot, 2 * PARTS + 2], o_sem.at[at], {"pp": i // per_stage})
 
     def sent_on(i):
         @pl.when(stage < last)
         def _():
             for c in next_copies(i):
                 c.wait_send()
+
+            @pl.when((stage == 0) & (i == 0))
+            def _():
+                for c in straight_copies():
+                    c.wait_send()
 
         pl.when((stage == last) & (i < per_stage * last))(lambda: out_copy(i).wait_send())
 
@@ -328,11 +519,11 @@
         slot = lax.rem(i, 2)
         pl.when(i >= 2)(lambda: sent_on(i - 2))
         own = rows_of(me, shard)
-        for c in range(2):
+        for c in range(len(cuts)):
             copies = scatter(i, c)
             for copy in copies:
                 copy.wait_recv()
-            cols = pl.ds(c * half, half)
+            cols = cuts[c]
             m = part[slot, own, cols].astype(F32)
             for k in range(3):
                 m = m + fin[slot, k, :, cols].astype(F32)
@@ -346,6 +537,11 @@
                 for k in range(3):
                     pl.semaphore_wait(free_sem.at[k], 1)
 
+            @pl.when((stage == 0) & (i == 0))
+            def _():
+                for c in straight_copies():
+                    c.start()
+
             for c in next_copies(i):
                 c.start()
 
@@ -355,43 +551,115 @@
         def _():
             obuf[lax.rem(i, per_stage)] = x2[slot]
 
-        for c in range(2):
+        for c in range(len(cuts)):
             for copy in scatter(i, c):
                 copy.wait_send()
 
+    load_out.wait()
+    even = lax.rem(stage, 2) == 0
+
     @pl.when(stage == 0)
     def _():
         begin(0)
+        whole_even.lend_all()
+        gather_x(0).forward()
+        whole_even.first.start()
         begin(1)
-
-    load_out.wait()
-
-    pl.when(lax.rem(stage, 2) == 1)(lambda: pl.semaphore_wait(turn_sem, 1))
-    gather_w.start()
-    gather_w.forward()
-    gather_w.near()
-    gather_w.far()
-    gather_w.sent()
-    pl.when(lax.rem(stage, 2) == 0)(lambda: signal(turn_sem, {"pp": stage + 1}))
+        whole_even.lent_all()
+        signal(turn_sem.at[1], {"pp": stage + 1})
+
+    @pl.when(stage == 1)
+    def _():
+        pl.semaphore_wait(turn_sem.at[1], 1)
+        whole_odd.lend_all()
+        pl.semaphore_wait(turn_sem.at[0], 1)
+        whole_odd.first.start()
+        whole_odd.first.forward()
+        whole_odd.lent_all()
+
+    @pl.when((stage > 1) & even)
+    def _():
+        w = whole_even
+        for p in range(2):
+            pl.when(helps(p))(lambda p=p: w.help_gather(p, True))
+        for g in (w.first, w.rest):
+            g.start()
+
+        @pl.when(helps(0) | helps(1))
+        def _():
+            for p in range(2):
+                pl.when(helps(p))(lambda p=p: w.help_end(p))
+            load_dn.start()
+            signal(turn_sem.at[2], {"pp": stage + 1})
+
+        for g in (w.first, w.rest):
+            g.forward()
+        for g in (w.first, w.rest):
+            g.finish()
+        signal(turn_sem.at[0], {"pp": stage + 1})
+
+    @pl.when((stage > 1) & ~even)
+    def _():
+        w = whole_odd
+        pl.when(stage == 3)(w.lend_all)
+        pl.when(stage == 3)(lambda: w.help_gather(1, False))
+        pl.when(stage == last)(lambda: w.help_gather(0, False))
+
+        @pl.when(stage == 5)
+        def _():
+            for p in range(2):
+                w.help_gather(p, True)
+
+        pl.semaphore_wait(turn_sem.at[0], 1)
+        w.first.start()
+        pl.when(stage != 3)(w.rest.start)
+        for p in range(2):
+            pl.when(helps(p))(lambda p=p: w.help_end(p))
+        load_dn.start()
+        w.first.forward()
+
+        @pl.when(stage != 3)
+        def _():
+            w.rest.forward()
+            w.first.finish()
+            w.rest.finish()
+
+        @pl.when(stage == 3)
+        def _():
+            w.lent_all()
+            w.end()
+
     load_qkv.wait()
     load_up.wait()
     load_dn.wait()
-    gather_x(0).forward()
+    pl.when(stage > 0)(lambda: gather_x(0).forward())
 
     def step(i, carry):
         here = i < num_micro
 
         @pl.when(here)
         def _():
+            slot_at(0, i)
             attention_part(i)
             out_own(i)
 
-        pl.when(i >= 1)(lambda: hand_on(i - 1))
-        pl.when(here)(lambda: gather_c(i).forward())
-        pl.when((stage == 0) & (i < num_micro - 2))(lambda: begin(i + 2))
-        pl.when(here)(lambda: mlp_first(i))
-        pl.when(i < num_micro - 1)(lambda: gather_x(i + 1).forward())
-        pl.when(here)(lambda: mlp_second(i))
+            @pl.when((stage == 0) & (i == 0))
+            def _():
+                whole_even.first.forward()
+
+            slot_at(2, i)
+
+        pl.when(i == num_micro)(lambda: hand_on(i - 1))
+
+        @pl.when(here)
+        def _():
+            gather_c(i).forward()
+            slot_at(3, i)
+            mlp_first(i)
+            slot_at(6, i)
+            mlp_second(i)
+            slot_at(8, i)
+
         return carry
 
     lax.fori_loop(0, num_micro + 1, step, 0)
@@ -450,18 +718,25 @@
                 pltpu.VMEM((2, rows, width), BF16),
                 pltpu.VMEM((per_stage, rows, width), BF16),
                 dma((4,)),
-                dma((6,)),
-                dma((6,)),
-                dma((4, 4)),
-                dma((4, 6)),
-                dma((4, 7)),
                 dma((2, 6)),
                 dma((2, 6)),
-                dma((2, 2, 3)),
-                dma((2, 2, 3)),
-                dma((2, 5)),
+                dma((2, 6)),
+                dma((2, 6)),
+                dma((2, 2)),
+                dma((2, 2)),
+                dma((2, 6)),
+                dma((2, 6)),
+                dma((4, 2 * PARTS + 2)),
+                dma((4, 4 * PARTS + 2)),
+                dma((4, 4 * PARTS + 3)),
+                dma((2, 4 * PARTS + 2)),
+                dma((2, 4 * PARTS + 2)),
+                dma((2, len(CUT_FIFTHS), 3)),
+                dma((2, len(CUT_FIFTHS), 3)),
+                dma((2 * PARTS,)),
+                dma((2, 2 * PARTS + 3)),
                 dma((per_stage,)),
-                pltpu.SemaphoreType.REGULAR,
+                pltpu.SemaphoreType.REGULAR((3,)),
                 pltpu.SemaphoreType.REGULAR((3,)),
             ],
             compiler_params=pltpu.CompilerParams(

time: 700 us -> 596 us (0.85)
  Pallas kernels: 698 us -> 594 us
    pallas_call x1, Pallas kernels: 698 us -> 594 us  [device_program(): pl.pallas_call(functools.partial(layer_kernel, num_stages, ring, head_dim...]
where the time goes in v3:
time: 596 us
  Pallas kernels  594 us (100%)
    pallas_call x1, Pallas kernels, device_program(): pl.pallas_call(functools.partial(layer_kernel, num_stages, ring, head_dim...  594 us

profile of v3, /device:TPU:103, one launch (start us, length us, event | category | flops | bytes accessed | tf_op | source)
XLA Modules:
  0.0 595.9 jit_solution(4531107408012396565)
XLA Ops:
  0.0 594.2 %layers.1 = bf16[2,32,2560]{2,1,0:T(8,128)(2,1)} custom-call(bf16[16,32,2560]{2,1,0:T(8,128)(2,1)} %bitcast.12, f32[1,2560]{1,0:T(1,128)} %g1_ref.1, f32[1,2560]{1,0:T(1,128)} %s1_ref.1, bf16[2560,1920]{1,0:T(8,128)(2,1)} %bitcast.10, f32[1,1920]{1,0:T(1,128)} %bqkv_ref.1, bf16[640,2560]{1,0:T(8,128)(2,1)} %bitcast.11, f32[1,2560]{1,0:T(1,128)} %bout_ref.1, ...), custom_call_target="tpu_custom_call" | custom-call | tf_op jit(solution)/shard_map/layers/pallas_call | solution.py:698
  594.2 1.7 copy.16

commit v4 on v3

--- a/solution.py
+++ b/solution.py
@@ -10,8 +10,8 @@
 LN_EPS = 1e-5
 MESH = pl.DeviceIdType.MESH
 PARTS = 2
-CUT_FIFTHS = (2, 2, 1)
-POINTS = {"H0": 2, "He": 2, "Ho": 2, "F0": 5, "Fe": 5, "Fo": 6, "f0": 6, "fe": 6, "fo": 6}
+CUT_FIFTHS = (2, 1, 2)
+POINTS = {"H0": 2, "He": 2, "Ho": 2, "F0": 6, "Fe": 5, "Fo": 6, "f0": 6, "fe": 6, "fo": 6}
 F32 = jnp.float32
 BF16 = jnp.bfloat16
 
@@ -285,7 +285,7 @@
 
     others = ((left, 0), (right, 1), (left, 1), (right, 0), (opp, 0), (opp, 1))
     whole_even = Whole(own_k // 2, own_k // 4)
-    whole_odd = Whole(own_k // 2, own_k // 4)
+    whole_odd = Whole(9 * own_k // 20, 11 * own_k // 40)
 
     def gather_c(i):
         slot = lax.rem(i, 2)
@@ -514,6 +514,15 @@
                     c.wait_send()
 
         pl.when((stage == last) & (i < per_stage * last))(lambda: out_copy(i).wait_send())
+
+    def later(i):
+        return (lax.rem(stage, 2) == 0) & (i < num_micro - 1)
+
+    def hand_on_rest(i):
+        @pl.when((stage < last) & later(i))
+        def _():
+            for c in next_copies(i)[2 * PARTS :]:
+                c.start()
 
     def hand_on(i):
         slot = lax.rem(i, 2)
@@ -542,8 +551,14 @@
                 for c in straight_copies():
                     c.start()
 
-            for c in next_copies(i):
+            copies = next_copies(i)
+            for c in copies[: 2 * PARTS]:
                 c.start()
+
+            @pl.when(~later(i))
+            def _():
+                for c in copies[2 * PARTS :]:
+                    c.start()
 
         pl.when((stage == last) & (i < per_stage * last))(lambda: out_copy(i).start())
 
@@ -654,6 +669,7 @@
         @pl.when(here)
         def _():
             gather_c(i).forward()
+            pl.when(i >= 1)(lambda: hand_on_rest(i - 1))
             slot_at(3, i)
             mlp_first(i)
             slot_at(6, i)

time: 596 us -> 587 us (0.985)
  Pallas kernels: 594 us -> 585 us
    pallas_call x1, Pallas kernels: 594 us -> 585 us  [device_program(): pl.pallas_call(functools.partial(layer_kernel, num_stages, ring, head_dim...]
where the time goes in v4:
time: 587 us
  Pallas kernels  585 us (100%)
    pallas_call x1, Pallas kernels, device_program(): pl.pallas_call(functools.partial(layer_kernel, num_stages, ring, head_dim...  585 us

profile of v4, /device:TPU:103, one launch (start us, length us, event | category | flops | bytes accessed | tf_op | source)
XLA Modules:
  0.0 586.6 jit_solution(10983457083540466482)
XLA Ops:
  0.0 584.9 %layers.1 = bf16[2,32,2560]{2,1,0:T(8,128)(2,1)} custom-call(bf16[16,32,2560]{2,1,0:T(8,128)(2,1)} %bitcast.12, f32[1,2560]{1,0:T(1,128)} %g1_ref.1, f32[1,2560]{1,0:T(1,128)} %s1_ref.1, bf16[2560,1920]{1,0:T(8,128)(2,1)} %bitcast.10, f32[1,1920]{1,0:T(1,128)} %bqkv_ref.1, bf16[640,2560]{1,0:T(8,128)(2,1)} %bitcast.11, f32[1,2560]{1,0:T(1,128)} %bout_ref.1, ...), custom_call_target="tpu_custom_call" | custom-call | tf_op jit(solution)/shard_map/layers/pallas_call | solution.py:714
  584.9 1.7 copy.16

commit v5 on v4

--- a/solution.py
+++ b/solution.py
@@ -10,7 +10,7 @@
 LN_EPS = 1e-5
 MESH = pl.DeviceIdType.MESH
 PARTS = 2
-CUT_FIFTHS = (2, 1, 2)
+CUT_FIFTHS = (1, 1, 1, 2)
 POINTS = {"H0": 2, "He": 2, "Ho": 2, "F0": 6, "Fe": 5, "Fo": 6, "f0": 6, "fe": 6, "fo": 6}
 F32 = jnp.float32
 BF16 = jnp.bfloat16

time: 587 us -> 587 us (level)
  no operation moved by 1% of the time
where the time goes in v5:
time: 587 us
  Pallas kernels  586 us (100%)
    pallas_call x1, Pallas kernels, device_program(): pl.pallas_call(functools.partial(layer_kernel, num_stages, ring, head_dim...  586 us

profile of v5, /device:TPU:103, one launch (start us, length us, event | category | flops | bytes accessed | tf_op | source)
XLA Modules:
  0.0 587.3 jit_solution(5258968847150064127)
XLA Ops:
  0.0 585.6 %layers.1 = bf16[2,32,2560]{2,1,0:T(8,128)(2,1)} custom-call(bf16[16,32,2560]{2,1,0:T(8,128)(2,1)} %bitcast.12, f32[1,2560]{1,0:T(1,128)} %g1_ref.1, f32[1,2560]{1,0:T(1,128)} %s1_ref.1, bf16[2560,1920]{1,0:T(8,128)(2,1)} %bitcast.10, f32[1,1920]{1,0:T(1,128)} %bqkv_ref.1, bf16[640,2560]{1,0:T(8,128)(2,1)} %bitcast.11, f32[1,2560]{1,0:T(1,128)} %bout_ref.1, ...), custom_call_target="tpu_custom_call" | custom-call | tf_op jit(solution)/shard_map/layers/pallas_call | solution.py:714
  585.6 1.7 copy.16
